TPU v7x, 128 devices: a whole 4x4x4 slice. The times are simulated.
128 devices in a mesh: batch: 1, cols: 16 (over z, y), rows: 8 (over x, core).
Axes of the slice: x: 4, y: 4, z: 4, core: 2. Of those that a mesh axis runs over, the one named last changes fastest.
Arguments:
- frames: bfloat16 [6, 1, 128, 1024, 256], P(None, 'batch', 'rows', 'cols')
- h_init: float32 [1, 128, 1024, 128], P('batch', 'rows', 'cols')
- w_x: bfloat16 [3, 3, 256, 384], replicated
- w_hzr: bfloat16 [3, 3, 128, 256], replicated
- w_hn: bfloat16 [3, 3, 128, 128], replicated
- gate_bias: float32 [384], replicated
Outputs:
- output 1: bfloat16 [6, 1, 128, 1024, 128], P(None, 'batch', 'rows', 'cols')
- output 2: float32 [1, 128, 1024, 128], P('batch', 'rows', 'cols')
All inputs are finite; a program needn't handle non-finite values.
Results may differ from a plain program's by a relative error of at most 0.00239247.
Values are sent between devices in bfloat16 or wider.
A program may use at most 1 GiB of HBM per device.

v0:
```python
import jax
import jax.numpy as jnp
from jax import lax
from jax.sharding import PartitionSpec as P, NamedSharding


def with_halo(tile, width, n_rows, n_cols):
    tile_h = tile.shape[-3]
    tile_w = tile.shape[-2]
    down_pairs = [(dev_idx, dev_idx + 1) for dev_idx in range(n_rows - 1)]
    up_pairs = [(dev_idx + 1, dev_idx) for dev_idx in range(n_rows - 1)]
    from_above = lax.ppermute(tile[..., tile_h - width:, :, :], 'rows', down_pairs)
    from_below = lax.ppermute(tile[..., :width, :, :], 'rows', up_pairs)
    tall_tile = jnp.concatenate([from_above, tile, from_below], axis=-3)
    right_pairs = [(dev_idx, dev_idx + 1) for dev_idx in range(n_cols - 1)]
    left_pairs = [(dev_idx + 1, dev_idx) for dev_idx in range(n_cols - 1)]
    from_left = lax.ppermute(tall_tile[..., tile_w - width:, :], 'cols', right_pairs)
    from_right = lax.ppermute(tall_tile[..., :width, :], 'cols', left_pairs)
    return jnp.concatenate([from_left, tall_tile, from_right], axis=-2)


def im2col_conv(padded, w_mat):
    out_h = padded.shape[-3] - 2
    out_w = padded.shape[-2] - 2
    tap_list = [padded[..., row_off:row_off + out_h, col_off:col_off + out_w, :] for row_off in range(3) for col_off in range(3)]
    patches = jnp.concatenate(tap_list, axis=-1)
    return jnp.einsum('...k,kg->...g', patches, w_mat, preferred_element_type=jnp.float32)


def solution(mesh):
    n_rows = mesh.shape['rows']
    n_cols = mesh.shape['cols']
    frame_spec = P(None, 'batch', 'rows', 'cols', None)
    state_spec = P('batch', 'rows', 'cols', None)

    def local_fn(frames, h_init, w_x, w_hzr, w_hn, gate_bias):
        n_hidden = h_init.shape[-1]
        wx_mat = w_x.reshape(-1, w_x.shape[-1])
        whzr_mat = w_hzr.reshape(-1, w_hzr.shape[-1])
        whn_mat = w_hn.reshape(-1, w_hn.shape[-1])
        frames_pad = with_halo(frames, 1, n_rows, n_cols)

        def one_step(h_prev, frame_pad):
            gate_x = im2col_conv(frame_pad, wx_mat) + gate_bias
            h_pad = with_halo(h_prev.astype(jnp.bfloat16), 1, n_rows, n_cols)
            zr_gates = jax.nn.sigmoid(gate_x[..., :2 * n_hidden] + im2col_conv(h_pad, whzr_mat))
            update = zr_gates[..., :n_hidden]
            reset_pad = with_halo((zr_gates[..., n_hidden:] * h_prev).astype(jnp.bfloat16), 1, n_rows, n_cols)
            candidate = jnp.tanh(gate_x[..., 2 * n_hidden:] + im2col_conv(reset_pad, whn_mat))
            h_next = (1.0 - update) * candidate + update * h_prev
            return h_next, h_next.astype(jnp.bfloat16)

        h_last, h_seq = lax.scan(one_step, h_init, frames_pad)
        return h_seq, h_last

    return jax.shard_map(local_fn, mesh=mesh, in_specs=(frame_spec, state_spec, P(), P(), P(), P()), out_specs=(frame_spec, state_spec), check_vma=False)
```

profile of v0, /device:TPU:99, one launch (start us, length us, event | category | flops | bytes accessed | tf_op | source)
XLA Modules:
  0.0 277.9 jit_solution(8818824812401801076)
XLA Ops:
  1.7 3.7 %collective-permute-start.8 = (bf16[6,1,1,64,256]{4,3,2,1,0:T(8,128)(2,1)S(1)}, bf16[6,1,1,64,256]{4,3,2,1,0:T(8,128)(2,1)S(1)}, u32[]{:S(2)}, u32[]{:S(2)}) collective-permute-start(bf16[6,1,1,64,256]{4,3,2,1,0:T(8,128)(2,1)S(1)} %get-tuple-element.80), channel_id=1, source_target_pairs={{0,1},{1,2},{2,3},{3,4},{4,5},{5,6},{6,7},{8,9},{9,10},{10,11},{11... | collective-permute-start | bytes 589832 | tf_op jit(solution)/shard_map/ppermute | solution.py:12
  17.5 4.2 %collective-permute-start.11 = (bf16[6,1,18,1,256]{4,3,2,1,0:T(2,128)(2,1)S(1)}, bf16[6,1,18,1,256]{4,3,2,1,0:T(2,128)(2,1)S(1)}, u32[]{:S(2)}, u32[]{:S(2)}) collective-permute-start(bf16[6,1,18,1,256]{4,3,2,1,0:T(2,128)(2,1)S(1)} %get-tuple-element.78), channel_id=1, source_target_pairs={{8,0},{16,8},{24,16},{32,24},{40,32},{48,40},{56,48},{64,56},{72,6... | collective-permute-start | bytes 165896 | tf_op jit(solution)/shard_map/ppermute | solution.py:18
  24.5 5.1 %pad_maximum_fusion.12 = bf16[6,1,18,66,256]{4,3,2,1,0:T(8,128)(2,1)} fusion(bf16[6,1,18,1,256]{4,3,2,1,0:T(2,128)(2,1)S(1)} %collective-permute-done.11, bf16[6,1,18,64,256]{4,3,2,1,0:T(8,128)(2,1)} %copy-done.3, bf16[6,1,18,1,256]{4,3,2,1,0:T(2,128)(2,1)S(1)} %collective-permute-done.10), kind=kLoop, calls=%fused_computation.66 | loop fusion | flops 10948608 | bytes 7299072 | tf_op jit(solution)/shard_map/concatenate | solution.py:19
  29.6 247.5 %while.12 = (s32[]{:T(128)}, f32[1,16,64,128]{3,2,1,0:T(8,128)S(1)}, bf16[6,1,16,64,128]{4,3,2,1,0:T(8,128)(2,1)}, bf16[6,1,18,66,256]{4,3,2,1,0:T(8,128)(2,1)},...) while((s32[]{:T(128)}, ...), condition=%wide.region_1.2_spmd, body=%wide.region_0.1_spmd.sunk | while | flops 2727606272 | bytes 56889316 | solution.py:53
  37.7 6.2 %collective-permute-start.2 = (bf16[1,18,1,128]{3,2,1,0:T(2,128)(2,1)S(1)}, bf16[1,18,1,128]{3,2,1,0:T(2,128)(2,1)S(1)}, u32[]{:S(2)}, u32[]{:S(2)}) collective-permute-start(bf16[1,18,1,128]{3,2,1,0:T(2,128)(2,1)S(1)} %get-tuple-element.146), channel_id=1, source_target_pairs={{8,0},{16,8},{24,16},{32,24},{40,32},{48,40},{56,48},{64,56},{72,6... | collective-permute-start | bytes 13832 | tf_op jit(solution)/shard_map/while/body/eval_jaxpr/ppermute | solution.py:18
  64.6 4.5 %collective-permute-done.7 = bf16[1,18,1,128]{3,2,1,0:T(2,128)(2,1)S(1)} collective-permute-done((bf16[1,18,1,128]{3,2,1,0:T(2,128)(2,1)S(1)}, bf16[1,18,1,128]{3,2,1,0:T(2,128)(2,1)S(1)}, u32[]{:S(2)}, u32[]{:S(2)}) %collective-permute-start.7) | collective-permute-done | bytes 4640 | tf_op jit(solution)/shard_map/while/body/eval_jaxpr/ppermute | solution.py:17
  72.9 4.4 %collective-permute-start = (bf16[1,1,64,128]{3,2,1,0:T(8,128)(2,1)S(1)}, bf16[1,1,64,128]{3,2,1,0:T(8,128)(2,1)S(1)}, u32[]{:S(2)}, u32[]{:S(2)}) collective-permute-start(bf16[1,1,64,128]{3,2,1,0:T(8,128)(2,1)S(1)} %get-tuple-element.144), channel_id=1, source_target_pairs={{1,0},{2,1},{3,2},{4,3},{5,4},{6,5},{7,6},{9,8},{10,9},{11,10},{12... | collective-permute-start | bytes 49160 | tf_op jit(solution)/shard_map/while/body/eval_jaxpr/ppermute | solution.py:13
  84.8 3.4 %collective-permute-start.3 = (bf16[1,18,1,128]{3,2,1,0:T(2,128)(2,1)S(1)}, bf16[1,18,1,128]{3,2,1,0:T(2,128)(2,1)S(1)}, u32[]{:S(2)}, u32[]{:S(2)}) collective-permute-start(bf16[1,18,1,128]{3,2,1,0:T(2,128)(2,1)S(1)} %get-tuple-element.147), channel_id=1, source_target_pairs={{0,8},{8,16},{16,24},{24,32},{32,40},{40,48},{48,56},{56,64},{64,7... | collective-permute-start | bytes 13832 | tf_op jit(solution)/shard_map/while/body/eval_jaxpr/ppermute | solution.py:17
  100.1 3.4 %collective-permute-start.6 = (bf16[1,18,1,128]{3,2,1,0:T(2,128)(2,1)S(1)}, bf16[1,18,1,128]{3,2,1,0:T(2,128)(2,1)S(1)}, u32[]{:S(2)}, u32[]{:S(2)}) collective-permute-start(bf16[1,18,1,128]{3,2,1,0:T(2,128)(2,1)S(1)} %get-tuple-element.152), channel_id=1, source_target_pairs={{8,0},{16,8},{24,16},{32,24},{40,32},{48,40},{56,48},{64,56},{72,6... | collective-permute-start | bytes 13832 | tf_op jit(solution)/shard_map/while/body/eval_jaxpr/ppermute | solution.py:18
  105.4 4.6 %collective-permute-done.7 = bf16[1,18,1,128]{3,2,1,0:T(2,128)(2,1)S(1)} collective-permute-done((bf16[1,18,1,128]{3,2,1,0:T(2,128)(2,1)S(1)}, bf16[1,18,1,128]{3,2,1,0:T(2,128)(2,1)S(1)}, u32[]{:S(2)}, u32[]{:S(2)}) %collective-permute-start.7) | collective-permute-done | bytes 4640 | tf_op jit(solution)/shard_map/while/body/eval_jaxpr/ppermute | solution.py:17
  113.7 4.4 %collective-permute-start = (bf16[1,1,64,128]{3,2,1,0:T(8,128)(2,1)S(1)}, bf16[1,1,64,128]{3,2,1,0:T(8,128)(2,1)S(1)}, u32[]{:S(2)}, u32[]{:S(2)}) collective-permute-start(bf16[1,1,64,128]{3,2,1,0:T(8,128)(2,1)S(1)} %get-tuple-element.144), channel_id=1, source_target_pairs={{1,0},{2,1},{3,2},{4,3},{5,4},{6,5},{7,6},{9,8},{10,9},{11,10},{12... | collective-permute-start | bytes 49160 | tf_op jit(solution)/shard_map/while/body/eval_jaxpr/ppermute | solution.py:13
  125.7 3.4 %collective-permute-start.3 = (bf16[1,18,1,128]{3,2,1,0:T(2,128)(2,1)S(1)}, bf16[1,18,1,128]{3,2,1,0:T(2,128)(2,1)S(1)}, u32[]{:S(2)}, u32[]{:S(2)}) collective-permute-start(bf16[1,18,1,128]{3,2,1,0:T(2,128)(2,1)S(1)} %get-tuple-element.147), channel_id=1, source_target_pairs={{0,8},{8,16},{16,24},{24,32},{32,40},{40,48},{48,56},{56,64},{64,7... | collective-permute-start | bytes 13832 | tf_op jit(solution)/shard_map/while/body/eval_jaxpr/ppermute | solution.py:17
  140.9 3.4 %collective-permute-start.6 = (bf16[1,18,1,128]{3,2,1,0:T(2,128)(2,1)S(1)}, bf16[1,18,1,128]{3,2,1,0:T(2,128)(2,1)S(1)}, u32[]{:S(2)}, u32[]{:S(2)}) collective-permute-start(bf16[1,18,1,128]{3,2,1,0:T(2,128)(2,1)S(1)} %get-tuple-element.152), channel_id=1, source_target_pairs={{8,0},{16,8},{24,16},{32,24},{40,32},{48,40},{56,48},{64,56},{72,6... | collective-permute-start | bytes 13832 | tf_op jit(solution)/shard_map/while/body/eval_jaxpr/ppermute | solution.py:18
  146.3 4.6 %collective-permute-done.7 = bf16[1,18,1,128]{3,2,1,0:T(2,128)(2,1)S(1)} collective-permute-done((bf16[1,18,1,128]{3,2,1,0:T(2,128)(2,1)S(1)}, bf16[1,18,1,128]{3,2,1,0:T(2,128)(2,1)S(1)}, u32[]{:S(2)}, u32[]{:S(2)}) %collective-permute-start.7) | collective-permute-done | bytes 4640 | tf_op jit(solution)/shard_map/while/body/eval_jaxpr/ppermute | solution.py:17
  154.6 4.4 %collective-permute-start = (bf16[1,1,64,128]{3,2,1,0:T(8,128)(2,1)S(1)}, bf16[1,1,64,128]{3,2,1,0:T(8,128)(2,1)S(1)}, u32[]{:S(2)}, u32[]{:S(2)}) collective-permute-start(bf16[1,1,64,128]{3,2,1,0:T(8,128)(2,1)S(1)} %get-tuple-element.144), channel_id=1, source_target_pairs={{1,0},{2,1},{3,2},{4,3},{5,4},{6,5},{7,6},{9,8},{10,9},{11,10},{12... | collective-permute-start | bytes 49160 | tf_op jit(solution)/shard_map/while/body/eval_jaxpr/ppermute | solution.py:13
  181.8 3.4 %collective-permute-start.6 = (bf16[1,18,1,128]{3,2,1,0:T(2,128)(2,1)S(1)}, bf16[1,18,1,128]{3,2,1,0:T(2,128)(2,1)S(1)}, u32[]{:S(2)}, u32[]{:S(2)}) collective-permute-start(bf16[1,18,1,128]{3,2,1,0:T(2,128)(2,1)S(1)} %get-tuple-element.152), channel_id=1, source_target_pairs={{8,0},{16,8},{24,16},{32,24},{40,32},{48,40},{56,48},{64,56},{72,6... | collective-permute-start | bytes 13832 | tf_op jit(solution)/shard_map/while/body/eval_jaxpr/ppermute | solution.py:18
  187.1 4.6 %collective-permute-done.7 = bf16[1,18,1,128]{3,2,1,0:T(2,128)(2,1)S(1)} collective-permute-done((bf16[1,18,1,128]{3,2,1,0:T(2,128)(2,1)S(1)}, bf16[1,18,1,128]{3,2,1,0:T(2,128)(2,1)S(1)}, u32[]{:S(2)}, u32[]{:S(2)}) %collective-permute-start.7) | collective-permute-done | bytes 4640 | tf_op jit(solution)/shard_map/while/body/eval_jaxpr/ppermute | solution.py:17
  195.5 4.4 %collective-permute-start = (bf16[1,1,64,128]{3,2,1,0:T(8,128)(2,1)S(1)}, bf16[1,1,64,128]{3,2,1,0:T(8,128)(2,1)S(1)}, u32[]{:S(2)}, u32[]{:S(2)}) collective-permute-start(bf16[1,1,64,128]{3,2,1,0:T(8,128)(2,1)S(1)} %get-tuple-element.144), channel_id=1, source_target_pairs={{1,0},{2,1},{3,2},{4,3},{5,4},{6,5},{7,6},{9,8},{10,9},{11,10},{12... | collective-permute-start | bytes 49160 | tf_op jit(solution)/shard_map/while/body/eval_jaxpr/ppermute | solution.py:13
  207.4 3.4 %collective-permute-start.3 = (bf16[1,18,1,128]{3,2,1,0:T(2,128)(2,1)S(1)}, bf16[1,18,1,128]{3,2,1,0:T(2,128)(2,1)S(1)}, u32[]{:S(2)}, u32[]{:S(2)}) collective-permute-start(bf16[1,18,1,128]{3,2,1,0:T(2,128)(2,1)S(1)} %get-tuple-element.147), channel_id=1, source_target_pairs={{0,8},{8,16},{16,24},{24,32},{32,40},{40,48},{48,56},{56,64},{64,7... | collective-permute-start | bytes 13832 | tf_op jit(solution)/shard_map/while/body/eval_jaxpr/ppermute | solution.py:17
  222.7 3.4 %collective-permute-start.6 = (bf16[1,18,1,128]{3,2,1,0:T(2,128)(2,1)S(1)}, bf16[1,18,1,128]{3,2,1,0:T(2,128)(2,1)S(1)}, u32[]{:S(2)}, u32[]{:S(2)}) collective-permute-start(bf16[1,18,1,128]{3,2,1,0:T(2,128)(2,1)S(1)} %get-tuple-element.152), channel_id=1, source_target_pairs={{8,0},{16,8},{24,16},{32,24},{40,32},{48,40},{56,48},{64,56},{72,6... | collective-permute-start | bytes 13832 | tf_op jit(solution)/shard_map/while/body/eval_jaxpr/ppermute | solution.py:18
  228.0 4.6 %collective-permute-done.7 = bf16[1,18,1,128]{3,2,1,0:T(2,128)(2,1)S(1)} collective-permute-done((bf16[1,18,1,128]{3,2,1,0:T(2,128)(2,1)S(1)}, bf16[1,18,1,128]{3,2,1,0:T(2,128)(2,1)S(1)}, u32[]{:S(2)}, u32[]{:S(2)}) %collective-permute-start.7) | collective-permute-done | bytes 4640 | tf_op jit(solution)/shard_map/while/body/eval_jaxpr/ppermute | solution.py:17
  236.3 4.4 %collective-permute-start = (bf16[1,1,64,128]{3,2,1,0:T(8,128)(2,1)S(1)}, bf16[1,1,64,128]{3,2,1,0:T(8,128)(2,1)S(1)}, u32[]{:S(2)}, u32[]{:S(2)}) collective-permute-start(bf16[1,1,64,128]{3,2,1,0:T(8,128)(2,1)S(1)} %get-tuple-element.144), channel_id=1, source_target_pairs={{1,0},{2,1},{3,2},{4,3},{5,4},{6,5},{7,6},{9,8},{10,9},{11,10},{12... | collective-permute-start | bytes 49160 | tf_op jit(solution)/shard_map/while/body/eval_jaxpr/ppermute | solution.py:13
  263.5 3.4 %collective-permute-start.6 = (bf16[1,18,1,128]{3,2,1,0:T(2,128)(2,1)S(1)}, bf16[1,18,1,128]{3,2,1,0:T(2,128)(2,1)S(1)}, u32[]{:S(2)}, u32[]{:S(2)}) collective-permute-start(bf16[1,18,1,128]{3,2,1,0:T(2,128)(2,1)S(1)} %get-tuple-element.152), channel_id=1, source_target_pairs={{8,0},{16,8},{24,16},{32,24},{40,32},{48,40},{56,48},{64,56},{72,6... | collective-permute-start | bytes 13832 | tf_op jit(solution)/shard_map/while/body/eval_jaxpr/ppermute | solution.py:18
  268.9 4.6 %collective-permute-done.7 = bf16[1,18,1,128]{3,2,1,0:T(2,128)(2,1)S(1)} collective-permute-done((bf16[1,18,1,128]{3,2,1,0:T(2,128)(2,1)S(1)}, bf16[1,18,1,128]{3,2,1,0:T(2,128)(2,1)S(1)}, u32[]{:S(2)}, u32[]{:S(2)}) %collective-permute-start.7) | collective-permute-done | bytes 4640 | tf_op jit(solution)/shard_map/while/body/eval_jaxpr/ppermute | solution.py:17
  (358 shorter events, 179.0 us)
Async XLA Ops:
  5.4 7.0 %collective-permute-start.9 = (bf16[6,1,1,64,256]{4,3,2,1,0:T(8,128)(2,1)S(1)}, bf16[6,1,1,64,256]{4,3,2,1,0:T(8,128)(2,1)S(1)}, u32[]{:S(2)}, u32[]{:S(2)}) collective-permute-start(bf16[6,1,1,64,256]{4,3,2,1,0:T(8,128)(2,1)S(1)} %get-tuple-element.79), channel_id=1, source_target_pairs={{1,0},{2,1},{3,2},{4,3},{5,4},{6,5},{7,6},{9,8},{10,9},{11,10},{12... | collective-permute-start | bytes 589832 | tf_op jit(solution)/shard_map/ppermute | solution.py:13
  14.3 8.8 %collective-permute-start.10 = (bf16[6,1,18,1,256]{4,3,2,1,0:T(2,128)(2,1)S(1)}, bf16[6,1,18,1,256]{4,3,2,1,0:T(2,128)(2,1)S(1)}, u32[]{:S(2)}, u32[]{:S(2)}) collective-permute-start(bf16[6,1,18,1,256]{4,3,2,1,0:T(2,128)(2,1)S(1)} %get-tuple-element.77), channel_id=1, source_target_pairs={{0,8},{8,16},{16,24},{24,32},{32,40},{40,48},{48,56},{56,64},{64,7... | collective-permute-start | bytes 165896 | tf_op jit(solution)/shard_map/ppermute | solution.py:17
  17.5 7.0 %collective-permute-start.11 = (bf16[6,1,18,1,256]{4,3,2,1,0:T(2,128)(2,1)S(1)}, bf16[6,1,18,1,256]{4,3,2,1,0:T(2,128)(2,1)S(1)}, u32[]{:S(2)}, u32[]{:S(2)}) collective-permute-start(bf16[6,1,18,1,256]{4,3,2,1,0:T(2,128)(2,1)S(1)} %get-tuple-element.78), channel_id=1, source_target_pairs={{8,0},{16,8},{24,16},{32,24},{40,32},{48,40},{56,48},{64,56},{72,6... | collective-permute-start | bytes 165896 | tf_op jit(solution)/shard_map/ppermute | solution.py:18
  29.7 8.0 %collective-permute-start = (bf16[1,1,64,128]{3,2,1,0:T(8,128)(2,1)S(1)}, bf16[1,1,64,128]{3,2,1,0:T(8,128)(2,1)S(1)}, u32[]{:S(2)}, u32[]{:S(2)}) collective-permute-start(bf16[1,1,64,128]{3,2,1,0:T(8,128)(2,1)S(1)} %get-tuple-element.144), channel_id=1, source_target_pairs={{1,0},{2,1},{3,2},{4,3},{5,4},{6,5},{7,6},{9,8},{10,9},{11,10},{12... | collective-permute-start | bytes 49160 | tf_op jit(solution)/shard_map/while/body/eval_jaxpr/ppermute | solution.py:13
  37.7 10.8 %collective-permute-start.2 = (bf16[1,18,1,128]{3,2,1,0:T(2,128)(2,1)S(1)}, bf16[1,18,1,128]{3,2,1,0:T(2,128)(2,1)S(1)}, u32[]{:S(2)}, u32[]{:S(2)}) collective-permute-start(bf16[1,18,1,128]{3,2,1,0:T(2,128)(2,1)S(1)} %get-tuple-element.146), channel_id=1, source_target_pairs={{8,0},{16,8},{24,16},{32,24},{40,32},{48,40},{56,48},{64,56},{72,6... | collective-permute-start | bytes 13832 | tf_op jit(solution)/shard_map/while/body/eval_jaxpr/ppermute | solution.py:18
  44.0 6.5 %collective-permute-start.3 = (bf16[1,18,1,128]{3,2,1,0:T(2,128)(2,1)S(1)}, bf16[1,18,1,128]{3,2,1,0:T(2,128)(2,1)S(1)}, u32[]{:S(2)}, u32[]{:S(2)}) collective-permute-start(bf16[1,18,1,128]{3,2,1,0:T(2,128)(2,1)S(1)} %get-tuple-element.147), channel_id=1, source_target_pairs={{0,8},{8,16},{16,24},{24,32},{32,40},{40,48},{48,56},{56,64},{64,7... | collective-permute-start | bytes 13832 | tf_op jit(solution)/shard_map/while/body/eval_jaxpr/ppermute | solution.py:17
  62.6 6.5 %collective-permute-start.7 = (bf16[1,18,1,128]{3,2,1,0:T(2,128)(2,1)S(1)}, bf16[1,18,1,128]{3,2,1,0:T(2,128)(2,1)S(1)}, u32[]{:S(2)}, u32[]{:S(2)}) collective-permute-start(bf16[1,18,1,128]{3,2,1,0:T(2,128)(2,1)S(1)} %get-tuple-element.153), channel_id=1, source_target_pairs={{0,8},{8,16},{16,24},{24,32},{32,40},{40,48},{48,56},{56,64},{64,7... | collective-permute-start | bytes 13832 | tf_op jit(solution)/shard_map/while/body/eval_jaxpr/ppermute | solution.py:17
  72.9 10.0 %collective-permute-start = (bf16[1,1,64,128]{3,2,1,0:T(8,128)(2,1)S(1)}, bf16[1,1,64,128]{3,2,1,0:T(8,128)(2,1)S(1)}, u32[]{:S(2)}, u32[]{:S(2)}) collective-permute-start(bf16[1,1,64,128]{3,2,1,0:T(8,128)(2,1)S(1)} %get-tuple-element.144), channel_id=1, source_target_pairs={{1,0},{2,1},{3,2},{4,3},{5,4},{6,5},{7,6},{9,8},{10,9},{11,10},{12... | collective-permute-start | bytes 49160 | tf_op jit(solution)/shard_map/while/body/eval_jaxpr/ppermute | solution.py:13
  82.9 7.9 %collective-permute-start.2 = (bf16[1,18,1,128]{3,2,1,0:T(2,128)(2,1)S(1)}, bf16[1,18,1,128]{3,2,1,0:T(2,128)(2,1)S(1)}, u32[]{:S(2)}, u32[]{:S(2)}) collective-permute-start(bf16[1,18,1,128]{3,2,1,0:T(2,128)(2,1)S(1)} %get-tuple-element.146), channel_id=1, source_target_pairs={{8,0},{16,8},{24,16},{32,24},{40,32},{48,40},{56,48},{64,56},{72,6... | collective-permute-start | bytes 13832 | tf_op jit(solution)/shard_map/while/body/eval_jaxpr/ppermute | solution.py:18
  84.8 6.8 %collective-permute-start.3 = (bf16[1,18,1,128]{3,2,1,0:T(2,128)(2,1)S(1)}, bf16[1,18,1,128]{3,2,1,0:T(2,128)(2,1)S(1)}, u32[]{:S(2)}, u32[]{:S(2)}) collective-permute-start(bf16[1,18,1,128]{3,2,1,0:T(2,128)(2,1)S(1)} %get-tuple-element.147), channel_id=1, source_target_pairs={{0,8},{8,16},{16,24},{24,32},{32,40},{40,48},{48,56},{56,64},{64,7... | collective-permute-start | bytes 13832 | tf_op jit(solution)/shard_map/while/body/eval_jaxpr/ppermute | solution.py:17
  113.7 10.0 %collective-permute-start = (bf16[1,1,64,128]{3,2,1,0:T(8,128)(2,1)S(1)}, bf16[1,1,64,128]{3,2,1,0:T(8,128)(2,1)S(1)}, u32[]{:S(2)}, u32[]{:S(2)}) collective-permute-start(bf16[1,1,64,128]{3,2,1,0:T(8,128)(2,1)S(1)} %get-tuple-element.144), channel_id=1, source_target_pairs={{1,0},{2,1},{3,2},{4,3},{5,4},{6,5},{7,6},{9,8},{10,9},{11,10},{12... | collective-permute-start | bytes 49160 | tf_op jit(solution)/shard_map/while/body/eval_jaxpr/ppermute | solution.py:13
  123.8 7.9 %collective-permute-start.2 = (bf16[1,18,1,128]{3,2,1,0:T(2,128)(2,1)S(1)}, bf16[1,18,1,128]{3,2,1,0:T(2,128)(2,1)S(1)}, u32[]{:S(2)}, u32[]{:S(2)}) collective-permute-start(bf16[1,18,1,128]{3,2,1,0:T(2,128)(2,1)S(1)} %get-tuple-element.146), channel_id=1, source_target_pairs={{8,0},{16,8},{24,16},{32,24},{40,32},{48,40},{56,48},{64,56},{72,6... | collective-permute-start | bytes 13832 | tf_op jit(solution)/shard_map/while/body/eval_jaxpr/ppermute | solution.py:18
  125.7 6.8 %collective-permute-start.3 = (bf16[1,18,1,128]{3,2,1,0:T(2,128)(2,1)S(1)}, bf16[1,18,1,128]{3,2,1,0:T(2,128)(2,1)S(1)}, u32[]{:S(2)}, u32[]{:S(2)}) collective-permute-start(bf16[1,18,1,128]{3,2,1,0:T(2,128)(2,1)S(1)} %get-tuple-element.147), channel_id=1, source_target_pairs={{0,8},{8,16},{16,24},{24,32},{32,40},{40,48},{48,56},{56,64},{64,7... | collective-permute-start | bytes 13832 | tf_op jit(solution)/shard_map/while/body/eval_jaxpr/ppermute | solution.py:17
  144.3 6.5 %collective-permute-start.7 = (bf16[1,18,1,128]{3,2,1,0:T(2,128)(2,1)S(1)}, bf16[1,18,1,128]{3,2,1,0:T(2,128)(2,1)S(1)}, u32[]{:S(2)}, u32[]{:S(2)}) collective-permute-start(bf16[1,18,1,128]{3,2,1,0:T(2,128)(2,1)S(1)} %get-tuple-element.153), channel_id=1, source_target_pairs={{0,8},{8,16},{16,24},{24,32},{32,40},{40,48},{48,56},{56,64},{64,7... | collective-permute-start | bytes 13832 | tf_op jit(solution)/shard_map/while/body/eval_jaxpr/ppermute | solution.py:17
  154.6 10.0 %collective-permute-start = (bf16[1,1,64,128]{3,2,1,0:T(8,128)(2,1)S(1)}, bf16[1,1,64,128]{3,2,1,0:T(8,128)(2,1)S(1)}, u32[]{:S(2)}, u32[]{:S(2)}) collective-permute-start(bf16[1,1,64,128]{3,2,1,0:T(8,128)(2,1)S(1)} %get-tuple-element.144), channel_id=1, source_target_pairs={{1,0},{2,1},{3,2},{4,3},{5,4},{6,5},{7,6},{9,8},{10,9},{11,10},{12... | collective-permute-start | bytes 49160 | tf_op jit(solution)/shard_map/while/body/eval_jaxpr/ppermute | solution.py:13
  164.6 7.9 %collective-permute-start.2 = (bf16[1,18,1,128]{3,2,1,0:T(2,128)(2,1)S(1)}, bf16[1,18,1,128]{3,2,1,0:T(2,128)(2,1)S(1)}, u32[]{:S(2)}, u32[]{:S(2)}) collective-permute-start(bf16[1,18,1,128]{3,2,1,0:T(2,128)(2,1)S(1)} %get-tuple-element.146), channel_id=1, source_target_pairs={{8,0},{16,8},{24,16},{32,24},{40,32},{48,40},{56,48},{64,56},{72,6... | collective-permute-start | bytes 13832 | tf_op jit(solution)/shard_map/while/body/eval_jaxpr/ppermute | solution.py:18
  166.6 6.8 %collective-permute-start.3 = (bf16[1,18,1,128]{3,2,1,0:T(2,128)(2,1)S(1)}, bf16[1,18,1,128]{3,2,1,0:T(2,128)(2,1)S(1)}, u32[]{:S(2)}, u32[]{:S(2)}) collective-permute-start(bf16[1,18,1,128]{3,2,1,0:T(2,128)(2,1)S(1)} %get-tuple-element.147), channel_id=1, source_target_pairs={{0,8},{8,16},{16,24},{24,32},{32,40},{40,48},{48,56},{56,64},{64,7... | collective-permute-start | bytes 13832 | tf_op jit(solution)/shard_map/while/body/eval_jaxpr/ppermute | solution.py:17
  195.5 10.0 %collective-permute-start = (bf16[1,1,64,128]{3,2,1,0:T(8,128)(2,1)S(1)}, bf16[1,1,64,128]{3,2,1,0:T(8,128)(2,1)S(1)}, u32[]{:S(2)}, u32[]{:S(2)}) collective-permute-start(bf16[1,1,64,128]{3,2,1,0:T(8,128)(2,1)S(1)} %get-tuple-element.144), channel_id=1, source_target_pairs={{1,0},{2,1},{3,2},{4,3},{5,4},{6,5},{7,6},{9,8},{10,9},{11,10},{12... | collective-permute-start | bytes 49160 | tf_op jit(solution)/shard_map/while/body/eval_jaxpr/ppermute | solution.py:13
  205.5 7.9 %collective-permute-start.2 = (bf16[1,18,1,128]{3,2,1,0:T(2,128)(2,1)S(1)}, bf16[1,18,1,128]{3,2,1,0:T(2,128)(2,1)S(1)}, u32[]{:S(2)}, u32[]{:S(2)}) collective-permute-start(bf16[1,18,1,128]{3,2,1,0:T(2,128)(2,1)S(1)} %get-tuple-element.146), channel_id=1, source_target_pairs={{8,0},{16,8},{24,16},{32,24},{40,32},{48,40},{56,48},{64,56},{72,6... | collective-permute-start | bytes 13832 | tf_op jit(solution)/shard_map/while/body/eval_jaxpr/ppermute | solution.py:18
  207.4 6.8 %collective-permute-start.3 = (bf16[1,18,1,128]{3,2,1,0:T(2,128)(2,1)S(1)}, bf16[1,18,1,128]{3,2,1,0:T(2,128)(2,1)S(1)}, u32[]{:S(2)}, u32[]{:S(2)}) collective-permute-start(bf16[1,18,1,128]{3,2,1,0:T(2,128)(2,1)S(1)} %get-tuple-element.147), channel_id=1, source_target_pairs={{0,8},{8,16},{16,24},{24,32},{32,40},{40,48},{48,56},{56,64},{64,7... | collective-permute-start | bytes 13832 | tf_op jit(solution)/shard_map/while/body/eval_jaxpr/ppermute | solution.py:17
  226.1 6.5 %collective-permute-start.7 = (bf16[1,18,1,128]{3,2,1,0:T(2,128)(2,1)S(1)}, bf16[1,18,1,128]{3,2,1,0:T(2,128)(2,1)S(1)}, u32[]{:S(2)}, u32[]{:S(2)}) collective-permute-start(bf16[1,18,1,128]{3,2,1,0:T(2,128)(2,1)S(1)} %get-tuple-element.153), channel_id=1, source_target_pairs={{0,8},{8,16},{16,24},{24,32},{32,40},{40,48},{48,56},{56,64},{64,7... | collective-permute-start | bytes 13832 | tf_op jit(solution)/shard_map/while/body/eval_jaxpr/ppermute | solution.py:17
  236.3 10.0 %collective-permute-start = (bf16[1,1,64,128]{3,2,1,0:T(8,128)(2,1)S(1)}, bf16[1,1,64,128]{3,2,1,0:T(8,128)(2,1)S(1)}, u32[]{:S(2)}, u32[]{:S(2)}) collective-permute-start(bf16[1,1,64,128]{3,2,1,0:T(8,128)(2,1)S(1)} %get-tuple-element.144), channel_id=1, source_target_pairs={{1,0},{2,1},{3,2},{4,3},{5,4},{6,5},{7,6},{9,8},{10,9},{11,10},{12... | collective-permute-start | bytes 49160 | tf_op jit(solution)/shard_map/while/body/eval_jaxpr/ppermute | solution.py:13
  246.4 7.9 %collective-permute-start.2 = (bf16[1,18,1,128]{3,2,1,0:T(2,128)(2,1)S(1)}, bf16[1,18,1,128]{3,2,1,0:T(2,128)(2,1)S(1)}, u32[]{:S(2)}, u32[]{:S(2)}) collective-permute-start(bf16[1,18,1,128]{3,2,1,0:T(2,128)(2,1)S(1)} %get-tuple-element.146), channel_id=1, source_target_pairs={{8,0},{16,8},{24,16},{32,24},{40,32},{48,40},{56,48},{64,56},{72,6... | collective-permute-start | bytes 13832 | tf_op jit(solution)/shard_map/while/body/eval_jaxpr/ppermute | solution.py:18
  248.3 6.8 %collective-permute-start.3 = (bf16[1,18,1,128]{3,2,1,0:T(2,128)(2,1)S(1)}, bf16[1,18,1,128]{3,2,1,0:T(2,128)(2,1)S(1)}, u32[]{:S(2)}, u32[]{:S(2)}) collective-permute-start(bf16[1,18,1,128]{3,2,1,0:T(2,128)(2,1)S(1)} %get-tuple-element.147), channel_id=1, source_target_pairs={{0,8},{8,16},{16,24},{24,32},{32,40},{40,48},{48,56},{56,64},{64,7... | collective-permute-start | bytes 13832 | tf_op jit(solution)/shard_map/while/body/eval_jaxpr/ppermute | solution.py:17
  (46 other events, 234.1 us)
where the time goes:
time: 282 us; the launch traced here: 278 us
  starting transfers between devices  157 us (56%)
  waiting for transfers between devices  43.9 us (16%)
  matrix products  37.4 us (13%)
  local copies, waits for them, and re-layouts  27 us (10%)
  other arithmetic  9.88 us (4%)
    ppermute x13, starting transfers between devices, with_halo(): lax.ppermute(tile[..., tile_h - width:, :, :], 'rows', down_pairs)  41.9 us
    ppermute x13, starting transfers between devices, with_halo(): from_below = lax.ppermute(tile[..., :width, :, :], 'rows', up_pairs)  40.8 us
    ppermute x13, starting transfers between devices, with_halo(): from_right = lax.ppermute(tall_tile[..., :width, :], 'cols', left_pairs)  40.4 us
    dot_general x18, matrix products, im2col_conv(): jnp.einsum('...k,kg->...g', patches, w_mat, preferred_element_type=jnp.fl...  37.4 us
    ppermute x13, waiting for transfers between devices, with_halo(): lax.ppermute(tall_tile[..., tile_w - width:, :], 'cols', right_pairs)  34.7 us
    ppermute x13, starting transfers between devices, with_halo(): lax.ppermute(tall_tile[..., tile_w - width:, :], 'cols', right_pairs)  33.5 us
    while x138, local copies, waits for them, and re-layouts  11.4 us
    concatenate x13, other arithmetic, with_halo(): return jnp.concatenate([from_left, tall_tile, from_right], axis=-2)  6.94 us
  transfers between devices with their start and end apart: 52, of which 22 were waited for; matrix products, arithmetic and copies ran while one was open for 11% of the time, Pallas kernels for 0%

commit v1 on v0

v1 whole, which is shorter than its diff:
```python
import functools

import jax
import jax.numpy as jnp
from jax import lax
from jax.experimental import pallas as pl
from jax.experimental.pallas import tpu as pltpu
from jax.sharding import PartitionSpec as P

MESH = pl.DeviceIdType.MESH
F32 = jnp.float32
BF16 = jnp.bfloat16

CH, CIN, SIDE, EDGE, TALL, WIDE = 128, 256, 8, 16, 20, 64
PITCH = 80
BLOCKS = 22
HALF = 11 * PITCH
DIRS = [(dr, dc) for dr in (-1, 0, 1) for dc in (-1, 0, 1) if (dr, dc) != (0, 0)]
EVEN = (PITCH, 736)
ODD = (PITCH, 720)
PAIR = 8 * PITCH + 16
GATE_CHUNK, CAND_CHUNK, ZR_CHUNK, N_CHUNK = 352, 320, 240, 160


def kernel(n_rows, n_cols, steps, refresh, frames, h_init, w_x, w_hzr, w_hn, bias, h_seq, h_last,
           hf, hl, hr, fs, fl, fr, xf, fx, ub, rh, vb, zb, gz, gn, wx, wxn, wh, whn, whr, hs,
           sem_w, sem_f, sem_o, f_send, f_recv, h_send, h_recv):
    row = lax.axis_index('rows')
    col = lax.axis_index('cols')

    def exists(dr, dc):
        conds = []
        if dr:
            conds.append(row + dr >= 0 if dr < 0 else row + dr < n_rows)
        if dc:
            conds.append(col + dc >= 0 if dc < 0 else col + dc < n_cols)
        return conds[0] if len(conds) == 1 else jnp.logical_and(*conds)

    def peer(dr, dc):
        return {'rows': lax.rem(row + dr + n_rows, n_rows), 'cols': lax.rem(col + dc + n_cols, n_cols)}

    def local_copies():
        return [pltpu.make_async_copy(w_x, wx, sem_w.at[0]), pltpu.make_async_copy(w_hzr, wh, sem_w.at[1]),
                pltpu.make_async_copy(w_hn, whr, sem_w.at[2]),
                pltpu.make_async_copy(h_init.at[0], hf.at[0, 3:19, EDGE:PITCH, :], sem_w.at[3])]

    def frame_copy(t):
        return pltpu.make_async_copy(frames.at[t, 0], fs.at[t, 2:18], sem_f.at[t])

    frame_copy(0).start()
    for cp in local_copies():
        cp.start()
    for t in range(1, steps):
        frame_copy(t).start()

    for t in range(steps):
        hf[t, 0, 72:PITCH, :] = jnp.zeros((SIDE, CH), F32)
        hf[t, 1, 0:SIDE, :] = jnp.zeros((SIDE, CH), F32)
        hf[t, 21, SIDE:24, :] = jnp.zeros((EDGE, CH), F32)
    for half in range(2):
        xf[half, 72:88, :] = jnp.zeros((EDGE, CH), F32)
        xf[half, 21 * PITCH + SIDE:21 * PITCH + 24, :] = jnp.zeros((EDGE, CH), F32)

    @pl.when(row == 0)
    def _():
        for t in range(steps):
            hf[t, 1, SIDE:PITCH, :] = jnp.zeros((72, CH), F32)
            hf[t, 2, 0:PITCH, :] = jnp.zeros((PITCH, CH), F32)
            hf[t, 3, 0:SIDE, :] = jnp.zeros((SIDE, CH), F32)
            fs[t, 0:2] = jnp.zeros((2, WIDE, CIN), BF16)
            fl[t, 0:2] = jnp.zeros((2, SIDE, CIN), BF16)
            fr[t, 0:2] = jnp.zeros((2, SIDE, CIN), BF16)
        for s in range(2):
            hl[s, 0:2] = jnp.zeros((2, SIDE, CH), F32)
            hr[s, 0:2] = jnp.zeros((2, SIDE, CH), F32)

    @pl.when(row == n_rows - 1)
    def _():
        for t in range(steps):
            hf[t, 19, SIDE:PITCH, :] = jnp.zeros((72, CH), F32)
            hf[t, TALL, 0:PITCH, :] = jnp.zeros((PITCH, CH), F32)
            hf[t, 21, 0:SIDE, :] = jnp.zeros((SIDE, CH), F32)
            fs[t, 18:TALL] = jnp.zeros((2, WIDE, CIN), BF16)
            fl[t, 18:TALL] = jnp.zeros((2, SIDE, CIN), BF16)
            fr[t, 18:TALL] = jnp.zeros((2, SIDE, CIN), BF16)
        for s in range(2):
            hl[s, 18:TALL] = jnp.zeros((2, SIDE, CH), F32)
            hr[s, 18:TALL] = jnp.zeros((2, SIDE, CH), F32)

    @pl.when(col == 0)
    def _():
        for t in range(steps):
            fl[t] = jnp.zeros((TALL, SIDE, CIN), BF16)
        hl[...] = jnp.zeros((2, TALL, SIDE, CH), F32)

    @pl.when(col == n_cols - 1)
    def _():
        for t in range(steps):
            fr[t] = jnp.zeros((TALL, SIDE, CIN), BF16)
        hr[...] = jnp.zeros((2, TALL, SIDE, CH), F32)

    barrier = pltpu.get_barrier_semaphore()
    count = jnp.int32(0)
    for d in DIRS:
        here = exists(*d)
        count = count + jnp.where(here, 1, 0)

        @pl.when(here)
        def _(d=d):
            pl.semaphore_signal(barrier, inc=1, device_id=peer(*d), device_id_type=MESH)
    pl.semaphore_wait(barrier, count)

    src_y = {-1: slice(0, 2), 0: slice(0, EDGE), 1: slice(14, EDGE)}
    dst_y = {-1: slice(18, TALL), 0: slice(2, 18), 1: slice(0, 2)}

    def frame_xfer(t, i):
        dr, dc = DIRS[i]
        if dc == 0:
            src = frames.at[t, 0, src_y[dr]]
            dst = fs.at[t, dst_y[dr]]
        elif dc == -1:
            src = frames.at[t, 0, src_y[dr], 0:SIDE]
            dst = fr.at[t, dst_y[dr]]
        else:
            src = frames.at[t, 0, src_y[dr], 56:WIDE]
            dst = fl.at[t, dst_y[dr]]
        return pltpu.make_async_remote_copy(src, dst, f_send.at[t, i], f_recv.at[t, i], device_id=peer(dr, dc), device_id_type=MESH)

    def state_xfer(t, i, full, from_arg=False):
        dr, dc = DIRS[i]
        k_src = {-1: slice(3, 5), 0: slice(3, 19), 1: slice(17, 19)}[dr]
        y_src = src_y[dr]
        k_dst = {-1: slice(19, 21), 0: slice(3, 19), 1: slice(1, 3)}[dr]
        if full:
            slot = jnp.where(t == 0, 0, 1)
            if dc == 0:
                xs, dst = slice(EDGE, PITCH), hf.at[t, k_dst, EDGE:PITCH]
            elif dc == -1:
                xs, dst = slice(EDGE, 24), hr.at[slot, dst_y[dr]]
            else:
                xs, dst = slice(72, PITCH), hl.at[slot, dst_y[dr]]
            src = h_init.at[0, y_src, slice(xs.start - EDGE, xs.stop - EDGE)] if from_arg else hf.at[t, k_src, xs]
        else:
            flat = hf.at[t].reshape(BLOCKS * PITCH, CH)
            src = flat.at[pl.ds(PITCH * k_src.start + SIDE, 2 * PITCH)]
            dst = flat.at[pl.ds(PITCH * k_dst.start + SIDE, 2 * PITCH)]
        return pltpu.make_async_remote_copy(src, dst, h_send.at[t, i], h_recv.at[t, i], device_id=peer(dr, dc), device_id_type=MESH)

    def start_frames(t):
        for i, d in enumerate(DIRS):
            @pl.when(exists(*d))
            def _(i=i):
                frame_xfer(t, i).start()

    def wait_frames(t):
        for i, (dr, dc) in enumerate(DIRS):
            @pl.when(exists(dr, dc))
            def _(i=i):
                frame_xfer(t, i).wait_send()

            @pl.when(exists(-dr, -dc))
            def _(i=i):
                frame_xfer(t, i).wait_recv()

    def start_state(t, full, from_arg=False):
        for i, d in enumerate(DIRS):
            if full or d[1] == 0:
                @pl.when(exists(*d))
                def _(i=i):
                    state_xfer(t, i, full, from_arg).start()

    def wait_state(t, full):
        for i, (dr, dc) in enumerate(DIRS):
            if full or dc == 0:
                @pl.when(exists(dr, dc))
                def _(i=i):
                    state_xfer(t, i, full).wait_send()

                @pl.when(exists(-dr, -dc))
                def _(i=i):
                    state_xfer(t, i, full).wait_recv()

    start_frames(0)
    start_state(0, True, True)

    def start_rest(t, carry):
        start_frames(t)
        return carry

    lax.fori_loop(1, steps, start_rest, 0)

    for cp in local_copies():
        cp.wait()
    for c in range(3):
        for a in range(4):
            i = a * 3 + c
            wxn[i * CIN:(i + 1) * CIN, 0:CH] = wx[a * 3 + c, :, CIN:384] if a < 3 else jnp.zeros((CIN, CH), BF16)
            wxn[i * CIN:(i + 1) * CIN, CH:CIN] = wx[(a - 1) * 3 + c, :, CIN:384] if a > 0 else jnp.zeros((CIN, CH), BF16)
            whn[i * CH:(i + 1) * CH, 0:CH] = whr[a * 3 + c] if a < 3 else jnp.zeros((CH, CH), BF16)
            whn[i * CH:(i + 1) * CH, CH:CIN] = whr[(a - 1) * 3 + c] if a > 0 else jnp.zeros((CH, CH), BF16)

    tap_blocks = {0: [(1, -PITCH), (0, 0), (1, 0)], 1: [(0, 0), (1, 0), (0, PITCH)]}
    pair_blocks = [(0, PITCH), (1, PITCH), (0, 2 * PITCH), (1, 2 * PITCH)]

    def patches(ref, blocks, lo, size):
        return jnp.concatenate([ref[c, par, lo + off:lo + off + size, :] for par, off in blocks for c in range(3)], axis=1)

    def chunks(lo, size, step):
        n = size // step
        return [(lo + i * step, step if i < n - 1 else size - i * step) for i in range(n)]

    def paired(step):
        both = zip(chunks(*EVEN, step), chunks(*ODD, step))
        return [(par,) + c for pair in both for par, c in enumerate(pair)]

    def gate_conv(t):
        for k in range(1, 21):
            for half in range(2):
                lanes = slice(half * CH, half * CH + CH)
                xf[half, PITCH * k + EDGE:PITCH * k + PITCH, :] = fs[t, k - 1, :, lanes].astype(F32)
                xf[half, PITCH * k + SIDE:PITCH * k + EDGE, :] = fl[t, k - 1, :, lanes].astype(F32)
                xf[half, PITCH * k + PITCH:PITCH * k + 88, :] = fr[t, k - 1, :, lanes].astype(F32)
        for k in range(1, 22):
            width = PITCH if k < 21 else EDGE
            for half in range(2):
                for c in range(3):
                    fx[c, k % 2, (k // 2) * PITCH:(k // 2) * PITCH + width, half * CH:half * CH + CH] = (
                        xf[half, PITCH * k - 1 + c:PITCH * k - 1 + c + width, :].astype(BF16))
        bias_zr = bias[0:CIN][None, :]
        wzr = wx[:, :, 0:CIN].reshape(9 * CIN, CIN)
        for par, lo, size in paired(GATE_CHUNK):
                gz[par, lo:lo + size, :] = jnp.dot(patches(fx, tap_blocks[par], lo, size), wzr, preferred_element_type=F32) + bias_zr
        bias_n = jnp.concatenate([bias[CIN:384], bias[CIN:384]])[None, :]
        for lo, size in chunks(0, PAIR, CAND_CHUNK):
            gn[lo:lo + size, :] = jnp.dot(patches(fx, pair_blocks, lo, size), wxn[...], preferred_element_type=F32) + bias_n

    left_edge = col == 0
    right_edge = col == n_cols - 1

    def step(t, carry):
        frame_copy(t).wait()
        wait_frames(t)
        gate_conv(t)
        is_full = jnp.logical_or(t == 0, t == refresh)

        @pl.when(is_full)
        def _():
            wait_state(t, True)
            slot = jnp.where(t == 0, 0, 1)
            for y in range(TALL):
                hf[t, y + 1, SIDE:EDGE, :] = hl[slot, y]
                hf[t, y + 2, 0:SIDE, :] = hr[slot, y]

        @pl.when(jnp.logical_not(is_full))
        def _():
            wait_state(t, False)

        h_flat = hf.at[t].reshape(BLOCKS * PITCH, CH)
        for k in range(1, 22):
            width = PITCH if k < 21 else EDGE
            for c in range(3):
                ub[c, k % 2, (k // 2) * PITCH:(k // 2) * PITCH + width, :] = h_flat[PITCH * k - 1 + c:PITCH * k - 1 + c + width, :].astype(BF16)

        whzr = wh[...].reshape(9 * CH, CIN)
        for par, lo, size in paired(ZR_CHUNK):
                pre = jnp.dot(patches(ub, tap_blocks[par], lo, size), whzr, preferred_element_type=F32) + gz[par, lo:lo + size, :]
                gate = 0.5 * jnp.tanh(0.5 * pre) + 0.5
                zb[par, lo:lo + size, :] = gate[:, 0:CH]
                for s in range(0, size, PITCH):
                    k = 2 * ((lo + s) // PITCH) + par
                    width = min(PITCH, size - s)
                    rh[PITCH * k:PITCH * k + width, :] = gate[s:s + width, CH:CIN] * h_flat[PITCH * k:PITCH * k + width, :]
        for k in range(2, 21):
            width = PITCH if k < TALL else EDGE
            for c in range(3):
                vb[c, k % 2, (k // 2) * PITCH:(k // 2) * PITCH + width, :] = rh[PITCH * k - 1 + c:PITCH * k - 1 + c + width, :].astype(BF16)

        last = t == steps - 1
        next_full = t + 1 == refresh
        keep_border = jnp.logical_not(jnp.logical_or(last, next_full))
        for lo, size in chunks(0, PAIR, N_CHUNK):
            cand = jnp.tanh(jnp.dot(patches(vb, pair_blocks, lo, size), whn[...], preferred_element_type=F32) + gn[lo:lo + size, :])
            for s in range(0, size, PITCH):
                yy = (lo + s) // PITCH
                width = min(PITCH, size - s)
                for odd in range(2):
                    k = 2 * yy + 3 + odd
                    if width < PITCH and odd:
                        continue
                    z_lo = (k // 2) * PITCH
                    z = zb[k % 2, z_lo:z_lo + width, :]
                    h_new = (1.0 - z) * cand[s:s + width, odd * CH:odd * CH + CH] + z * h_flat[PITCH * k:PITCH * k + width, :]
                    if width == PITCH:
                        main = h_new[EDGE:PITCH]
                        hs[t, k - 3] = main.astype(BF16)
                        hf[t + 1, k, EDGE:PITCH, :] = main
                        hf[t + 1, k, SIDE:EDGE, :] = jnp.where(left_edge, 0.0, h_new[SIDE:EDGE])
                    if k > 3:
                        hf[t + 1, k, 0:SIDE, :] = jnp.where(right_edge, 0.0, h_new[0:SIDE])

        @pl.when(next_full)
        def _():
            start_state(t + 1, True)

        @pl.when(keep_border)
        def _():
            start_state(t + 1, False)

        pltpu.make_async_copy(hs.at[t], h_seq.at[t, 0], sem_o.at[t]).start()
        return carry

    for par, lo in ((1, 10 * PITCH), (0, 10 * PITCH)):
        for c in range(3):
            vb[c, par, lo:lo + EDGE, :] = jnp.zeros((EDGE, CH), BF16)
    rh[2 * PITCH - SIDE:2 * PITCH, :] = jnp.zeros((SIDE, CH), F32)
    rh[TALL * PITCH + EDGE:TALL * PITCH + 24, :] = jnp.zeros((SIDE, CH), F32)
    lax.fori_loop(0, steps, step, 0)
    last_copy = pltpu.make_async_copy(hf.at[steps, 3:19, EDGE:PITCH, :], h_last.at[0], sem_w.at[0])
    last_copy.start()
    for t in range(steps):
        pltpu.make_async_copy(hs.at[t], h_seq.at[t, 0], sem_o.at[t]).wait()
    last_copy.wait()


def solution(mesh):
    n_rows = mesh.shape['rows']
    n_cols = mesh.shape['cols']
    frame_spec = P(None, 'batch', 'rows', 'cols', None)
    state_spec = P('batch', 'rows', 'cols', None)

    def local_fn(frames, h_init, w_x, w_hzr, w_hn, gate_bias):
        steps = frames.shape[0]
        any_spec = pl.BlockSpec(memory_space=pl.ANY)
        vmem = pltpu.VMEM
        dma = pltpu.SemaphoreType.DMA
        return pl.pallas_call(
            functools.partial(kernel, n_rows, n_cols, steps, 3),
            out_shape=(jax.ShapeDtypeStruct((steps, 1, EDGE, WIDE, CH), BF16), jax.ShapeDtypeStruct((1, EDGE, WIDE, CH), F32)),
            in_specs=[any_spec] * 5 + [pl.BlockSpec(memory_space=pltpu.VMEM)],
            out_specs=(any_spec, any_spec),
            scratch_shapes=[
                vmem((steps + 1, BLOCKS, PITCH, CH), F32),
                vmem((2, TALL, SIDE, CH), F32),
                vmem((2, TALL, SIDE, CH), F32),
                vmem((steps, TALL, WIDE, CIN), BF16),
                vmem((steps, TALL, SIDE, CIN), BF16),
                vmem((steps, TALL, SIDE, CIN), BF16),
                vmem((2, BLOCKS * PITCH, CH), F32),
                vmem((3, 2, HALF, CIN), BF16),
                vmem((3, 2, HALF, CH), BF16),
                vmem((BLOCKS * PITCH, CH), F32),
                vmem((3, 2, HALF, CH), BF16),
                vmem((2, HALF, CH), F32),
                vmem((2, HALF, CIN), F32),
                vmem((PAIR, CIN), F32),
                vmem((9, CIN, 384), BF16),
                vmem((12 * CIN, CIN), BF16),
                vmem((9, CH, CIN), BF16),
                vmem((12 * CH, CIN), BF16),
                vmem((9, CH, CH), BF16),
                vmem((steps, EDGE, WIDE, CH), BF16),
                dma((4,)), dma((steps,)), dma((steps,)),
                dma((steps, SIDE)), dma((steps, SIDE)), dma((steps, SIDE)), dma((steps, SIDE)),
            ],
            compiler_params=pltpu.CompilerParams(collective_id=0, has_side_effects=True, vmem_limit_bytes=60 * 1024 * 1024),
        )(frames, h_init, w_x.reshape(9, CIN, 384), w_hzr.reshape(9, CH, CIN), w_hn.reshape(9, CH, CH), gate_bias)

    return jax.shard_map(local_fn, mesh=mesh, in_specs=(frame_spec, state_spec, P(), P(), P(), P()), out_specs=(frame_spec, state_spec), check_vma=False)
```

time: 282 us -> 49.6 us (0.18); the launches traced: 278 us -> 49.5 us
  starting transfers between devices: 157 us -> 0 us
  Pallas kernels: 0 us -> 45.2 us
  waiting for transfers between devices: 43.9 us -> 0 us
  matrix products: 37.4 us -> 0 us
  local copies, waits for them, and re-layouts: 27 us -> 3.61 us
  other arithmetic: 9.88 us -> 0 us
    ppermute x52 -> x0, starting transfers between devices: 157 us -> none  [the longest x13 41.9 us: with_halo(): lax.ppermute(tile[..., tile_h - width:, :, :], 'rows', down_pairs)]
    pallas_call x0 -> x1, Pallas kernels: none -> 45.2 us  [local_fn(): pl.pallas_call(functools.partial(kernel, n_rows, n_cols, steps, 3), out_s...]
    ppermute x52 -> x0, waiting for transfers between devices: 43.9 us -> none  [the longest x13 34.7 us: with_halo(): lax.ppermute(tall_tile[..., tile_w - width:, :], 'cols', right_pairs)]
    dot_general x18 -> x0, matrix products: 37.4 us -> none  [im2col_conv(): jnp.einsum('...k,kg->...g', patches, w_mat, preferred_element_type=jnp.fl...]
    while x138 -> x0, local copies, waits for them, and re-layouts: 11.4 us -> none
    concatenate x25 -> x0, other arithmetic: 7.18 us -> none  [the longest x13 6.94 us: with_halo(): return jnp.concatenate([from_left, tall_tile, from_right], axis=-2)]
    squeeze x6 -> x0, local copies, waits for them, and re-layouts: 6.84 us -> none  [local_fn(): h_last, h_seq = lax.scan(one_step, h_init, frames_pad)]
  transfers between devices with their start and end apart: 52 -> 0, of which waited for: 22 -> 0; matrix products, arithmetic and copies ran while one was open for 11% -> 0% of each run, Pallas kernels for 0% -> 0%
where the time goes in v1:
time: 49.6 us; the launch traced here: 49.5 us
  Pallas kernels  45.2 us (91%)
  local copies, waits for them, and re-layouts  3.61 us (7%)
  between operations  0.65 us (1%)
    pallas_call x1, Pallas kernels, local_fn(): pl.pallas_call(functools.partial(kernel, n_rows, n_cols, steps, 3), out_s...  45.2 us
    unnamed x4, local copies, waits for them, and re-layouts  3.61 us

profile of v1, /device:TPU:99, one launch (start us, length us, event | category | flops | bytes accessed | tf_op | source)
XLA Modules:
  0.0 49.5 jit_solution(5398037085891013965)
XLA Ops:
  0.6 45.2 %shard_map.77 = (bf16[6,1,16,64,128]{4,3,2,1,0:T(8,128)(2,1)}, f32[1,16,64,128]{3,2,1,0:T(8,128)}) custom-call(bf16[6,1,16,64,256]{4,3,2,1,0:T(8,128)(2,1)} %frames.1, f32[1,16,64,128]{3,2,1,0:T(8,128)} %h_init.1, bf16[9,256,384]{2,1,0:T(8,128)(2,1)} %bitcast.3, bf16[9,128,256]{2,1,0:T(8,128)(2,1)} %bitcast.4, bf16[9,128,128]{2,1,0:T(8,128)(2,1)} %bitcast.5, ...), custom_call_target="tpu_custom_call" | custom-call | tf_op jit(solution)/shard_map/pallas_call | solution.py:336
  45.8 0.0 copy-start
  45.8 2.8 %copy.10 = bf16[6,1,16,64,128]{4,3,2,1,0:T(8,128)(2,1)} copy(bf16[6,1,16,64,128]{4,3,2,1,0:T(8,128)(2,1)} %get-tuple-element.4) | data formatting | bytes 3145728
  48.7 0.0 copy-done
  48.7 0.8 %copy.11 = f32[1,16,64,128]{3,2,1,0:T(8,128)} copy(f32[1,16,64,128]{3,2,1,0:T(8,128)S(1)} %copy-done) | data formatting | bytes 1048576
Async XLA Ops:
  45.8 2.8 %copy-start = (f32[1,16,64,128]{3,2,1,0:T(8,128)S(1)}, f32[1,16,64,128]{3,2,1,0:T(8,128)}, u32[]{:S(2)}) copy-start(f32[1,16,64,128]{3,2,1,0:T(8,128)} %get-tuple-element.5) | copy-start | bytes 1572868

commit v2 on v1

--- a/solution.py
+++ b/solution.py
@@ -23,8 +23,8 @@
 
 
 def kernel(n_rows, n_cols, steps, refresh, frames, h_init, w_x, w_hzr, w_hn, bias, h_seq, h_last,
-           hf, hl, hr, fs, fl, fr, xf, fx, ub, rh, vb, zb, gz, gn, wx, wxn, wh, whn, whr, hs,
-           sem_w, sem_f, sem_o, f_send, f_recv, h_send, h_recv):
+           hf, hl, hr, fs, fl, fr, xf, fx, ub, rh, vb, zb, gz, gn, wx, wxn, wh, whn, whr,
+           sem_w, sem_f, f_send, f_recv, h_send, h_recv):
     row = lax.axis_index('rows')
     col = lax.axis_index('cols')
 
@@ -292,7 +292,8 @@
                     h_new = (1.0 - z) * cand[s:s + width, odd * CH:odd * CH + CH] + z * h_flat[PITCH * k:PITCH * k + width, :]
                     if width == PITCH:
                         main = h_new[EDGE:PITCH]
-                        hs[t, k - 3] = main.astype(BF16)
+                        h_seq[t, 0, k - 3] = main.astype(BF16)
+                        h_last[0, k - 3] = main
                         hf[t + 1, k, EDGE:PITCH, :] = main
                         hf[t + 1, k, SIDE:EDGE, :] = jnp.where(left_edge, 0.0, h_new[SIDE:EDGE])
                     if k > 3:
@@ -306,7 +307,6 @@
         def _():
             start_state(t + 1, False)
 
-        pltpu.make_async_copy(hs.at[t], h_seq.at[t, 0], sem_o.at[t]).start()
         return carry
 
     for par, lo in ((1, 10 * PITCH), (0, 10 * PITCH)):
@@ -315,11 +315,6 @@
     rh[2 * PITCH - SIDE:2 * PITCH, :] = jnp.zeros((SIDE, CH), F32)
     rh[TALL * PITCH + EDGE:TALL * PITCH + 24, :] = jnp.zeros((SIDE, CH), F32)
     lax.fori_loop(0, steps, step, 0)
-    last_copy = pltpu.make_async_copy(hf.at[steps, 3:19, EDGE:PITCH, :], h_last.at[0], sem_w.at[0])
-    last_copy.start()
-    for t in range(steps):
-        pltpu.make_async_copy(hs.at[t], h_seq.at[t, 0], sem_o.at[t]).wait()
-    last_copy.wait()
 
 
 def solution(mesh):
@@ -335,9 +330,9 @@
         dma = pltpu.SemaphoreType.DMA
         return pl.pallas_call(
             functools.partial(kernel, n_rows, n_cols, steps, 3),
-            out_shape=(jax.ShapeDtypeStruct((steps, 1, EDGE, WIDE, CH), BF16), jax.ShapeDtypeStruct((1, EDGE, WIDE, CH), F32)),
+            out_shape=(vmem((steps, 1, EDGE, WIDE, CH), BF16), vmem((1, EDGE, WIDE, CH), F32)),
             in_specs=[any_spec] * 5 + [pl.BlockSpec(memory_space=pltpu.VMEM)],
-            out_specs=(any_spec, any_spec),
+            out_specs=(pl.BlockSpec(memory_space=vmem), pl.BlockSpec(memory_space=vmem)),
             scratch_shapes=[
                 vmem((steps + 1, BLOCKS, PITCH, CH), F32),
                 vmem((2, TALL, SIDE, CH), F32),
@@ -358,8 +353,7 @@
                 vmem((9, CH, CIN), BF16),
                 vmem((12 * CH, CIN), BF16),
                 vmem((9, CH, CH), BF16),
-                vmem((steps, EDGE, WIDE, CH), BF16),
-                dma((4,)), dma((steps,)), dma((steps,)),
+                dma((4,)), dma((steps,)),
                 dma((steps, SIDE)), dma((steps, SIDE)), dma((steps, SIDE)), dma((steps, SIDE)),
             ],
             compiler_params=pltpu.CompilerParams(collective_id=0, has_side_effects=True, vmem_limit_bytes=60 * 1024 * 1024),

time: 49.6 us -> 46.9 us (0.946)
  local copies, waits for them, and re-layouts: 3.61 us -> 1.94 us
  Pallas kernels: 45.2 us -> 44.2 us
    unnamed x4 -> x2, local copies, waits for them, and re-layouts: 3.61 us -> 1.94 us
    pallas_call x1, Pallas kernels: 45.2 us -> 44.2 us  [local_fn(): pl.pallas_call(functools.partial(kernel, n_rows, n_cols, steps, 3), out_s...]
where the time goes in v2:
time: 46.9 us; the launch traced here: 46.7 us
  Pallas kernels  44.2 us (94%)
  local copies, waits for them, and re-layouts  1.94 us (4%)
  between operations  0.64 us (1%)
    pallas_call x1, Pallas kernels, local_fn(): pl.pallas_call(functools.partial(kernel, n_rows, n_cols, steps, 3), out_s...  44.2 us
    unnamed x2, local copies, waits for them, and re-layouts  1.94 us

profile of v2, /device:TPU:99, one launch (start us, length us, event | category | flops | bytes accessed | tf_op | source)
XLA Modules:
  0.0 46.7 jit_solution(9932847036808766613)
XLA Ops:
  0.6 44.2 %shard_map.77 = (bf16[6,1,16,64,128]{4,3,2,1,0:T(8,128)(2,1)S(1)}, f32[1,16,64,128]{3,2,1,0:T(8,128)S(1)}) custom-call(bf16[6,1,16,64,256]{4,3,2,1,0:T(8,128)(2,1)} %frames.1, f32[1,16,64,128]{3,2,1,0:T(8,128)} %h_init.1, bf16[9,256,384]{2,1,0:T(8,128)(2,1)} %bitcast.3, bf16[9,128,256]{2,1,0:T(8,128)(2,1)} %bitcast.4, bf16[9,128,128]{2,1,0:T(8,128)(2,1)} %bitcast.5, ...), custom_call_target="tpu_custom_call" | custom-call | tf_op jit(solution)/shard_map/pallas_call | solution.py:331
  44.8 1.1 %copy.10 = bf16[6,1,16,64,128]{4,3,2,1,0:T(8,128)(2,1)} copy(bf16[6,1,16,64,128]{4,3,2,1,0:T(8,128)(2,1)S(1)} %get-tuple-element.2) | data formatting | bytes 3145728
  45.9 0.8 %copy.11 = f32[1,16,64,128]{3,2,1,0:T(8,128)} copy(f32[1,16,64,128]{3,2,1,0:T(8,128)S(1)} %get-tuple-element.3) | data formatting | bytes 1048576

commit v3 on v0

v3 whole, which is shorter than its diff:
```python
import functools

import jax
import jax.numpy as jnp
from jax import lax
from jax.experimental import pallas as pl
from jax.experimental.pallas import tpu as pltpu
from jax.sharding import PartitionSpec as P

MESH = pl.DeviceIdType.MESH
F32 = jnp.float32
BF16 = jnp.bfloat16

CH, CIN, SIDE, EDGE, TALL, WIDE = 128, 256, 8, 16, 20, 64
PITCH = 80
BLOCKS = 22
CELLS = BLOCKS * PITCH
BLOCK = 3
OUTER = (1, 2, 19, 20)
DIRS = [(dr, dc) for dr in (-1, 0, 1) for dc in (-1, 0, 1) if (dr, dc) != (0, 0)]

MID = (32, WIDE)
LOW = (0, 32)
HIGH = (WIDE, PITCH)
ALL = (0, PITCH)
TIP = (0, EDGE)
GATE_CORE = [[(4, 11) + MID], [(11, 18) + MID]]
GATE_RIM = [[(2, 4) + ALL, (4, 7) + LOW], [(7, 15) + LOW], [(15, 18) + LOW, (4, 14) + HIGH],
            [(13, 18) + HIGH, (18, 20) + ALL, (20, 21) + TIP]]
CAND_CORE = [[(1, 4) + MID], [(4, 7) + MID]]
CAND_RIM = [[(0, 1) + ALL, (1, 6) + LOW], [(6, 7) + LOW, (1, 7) + HIGH, (7, 8) + ALL, (8, 9) + LOW]]
ZR_CORE = [(336, 272), (608, 272), (880, 288), (1168, 288)]
ZR_RIM = [(160, 176), (1440, 176)]
N_CORE = [[(2, 4) + ALL, (4, 5, 0, 48)], [(4, 5, 32, PITCH), (5, 7) + ALL]]
N_RIM = [[(0, 1) + ALL, (1, 2, 0, 48)], [(1, 2, 48, PITCH), (7, 8) + ALL, (8, 9) + TIP]]


def kernel(n_rows, n_cols, steps, frames, h_init, w_x, w_hzr, w_hn, bias, h_seq, h_last,
           hf, hl, hr, fs, fl, fr, xf, fx, ub, rh, vb, zb, gz, gn, wx, wxn, wh, whn, whr,
           sem_w, sem_f, f_send, f_recv, h_send, h_recv):
    row = lax.axis_index('rows')
    col = lax.axis_index('cols')

    def exists(dr, dc):
        conds = []
        if dr:
            conds.append(row + dr >= 0 if dr < 0 else row + dr < n_rows)
        if dc:
            conds.append(col + dc >= 0 if dc < 0 else col + dc < n_cols)
        return conds[0] if len(conds) == 1 else jnp.logical_and(*conds)

    def peer(dr, dc):
        return {'rows': lax.rem(row + dr + n_rows, n_rows), 'cols': lax.rem(col + dc + n_cols, n_cols)}

    def local_copies():
        return [pltpu.make_async_copy(w_x, wx, sem_w.at[0]), pltpu.make_async_copy(w_hzr, wh, sem_w.at[1]),
                pltpu.make_async_copy(w_hn, whr, sem_w.at[2]),
                pltpu.make_async_copy(h_init.at[0], hf.at[0, 3:19, EDGE:PITCH, :], sem_w.at[3])]

    def frame_copy(t):
        return pltpu.make_async_copy(frames.at[t, 0], fs.at[t, 2:18], sem_f.at[t])

    frame_copy(0).start()
    weights = local_copies()
    weights[3].start()
    weights[0].start()
    for t in range(1, BLOCK):
        frame_copy(t).start()
    weights[1].start()
    weights[2].start()

    barrier = pltpu.get_barrier_semaphore()
    count = jnp.int32(0)
    for d in DIRS:
        here = exists(*d)
        count = count + jnp.where(here, 1, 0)

        @pl.when(here)
        def _(d=d):
            pl.semaphore_signal(barrier, inc=1, device_id=peer(*d), device_id_type=MESH)
    pl.semaphore_wait(barrier, count)

    src_y = {-1: slice(0, 2), 0: slice(0, EDGE), 1: slice(14, EDGE)}
    dst_y = {-1: slice(18, TALL), 0: slice(2, 18), 1: slice(0, 2)}

    def frame_xfer(t, i, local=False):
        dr, dc = DIRS[i]
        cells, land = {0: (slice(0, WIDE), fs), -1: (slice(0, SIDE), fr), 1: (slice(WIDE - SIDE, WIDE), fl)}[dc]
        y = src_y[dr]
        src = fs.at[t, slice(y.start + 2, y.stop + 2), cells] if local else frames.at[t, 0, y, cells]
        return pltpu.make_async_remote_copy(src, land.at[t, dst_y[dr]], f_send.at[t, i], f_recv.at[t, i],
                                            device_id=peer(dr, dc), device_id_type=MESH)

    def state_xfer(t, i, slot):
        dr, dc = DIRS[i]
        k_src = {-1: 3, 0: 3, 1: 17}[dr]
        k_dst = {-1: 19, 0: 3, 1: 1}[dr]
        n = 2 if dr else EDGE
        if slot is None:
            flat = hf.at[t].reshape(BLOCKS * PITCH, CH)
            src = flat.at[pl.ds(PITCH * k_src + SIDE, 2 * PITCH)]
            dst = flat.at[pl.ds(PITCH * k_dst + SIDE, 2 * PITCH)]
        else:
            cells = {0: slice(EDGE, PITCH), -1: slice(EDGE, EDGE + SIDE), 1: slice(PITCH - SIDE, PITCH)}[dc]
            src = hf.at[t, slice(k_src, k_src + n), cells]
            dst = {0: hf.at[t, slice(k_dst, k_dst + n), cells], -1: hr.at[slot, dst_y[dr]], 1: hl.at[slot, dst_y[dr]]}[dc]
        return pltpu.make_async_remote_copy(src, dst, h_send.at[t, i], h_recv.at[t, i], device_id=peer(dr, dc), device_id_type=MESH)

    def start(make, rows_only=False):
        for i, d in enumerate(DIRS):
            if d[1] == 0 or not rows_only:
                @pl.when(exists(*d))
                def _(i=i):
                    make(i).start()

    def finish(make, rows_only=False):
        for i, (dr, dc) in enumerate(DIRS):
            if dc == 0 or not rows_only:
                @pl.when(exists(dr, dc))
                def _(i=i):
                    make(i).wait_send()

                @pl.when(exists(-dr, -dc))
                def _(i=i):
                    make(i).wait_recv()

    frame_copy(0).wait()
    start(lambda i: frame_xfer(0, i, True))
    weights[3].wait()
    start(lambda i: state_xfer(0, i, 0))

    def start_rest(t, carry):
        start(lambda i: frame_xfer(t, i))
        return carry

    lax.fori_loop(1, steps, start_rest, 0)
    for t in range(BLOCK, steps):
        frame_copy(t).start()

    for t in range(steps):
        hf[t, 0, 72:PITCH, :] = jnp.zeros((SIDE, CH), F32)
        hf[t, 1, 0:SIDE, :] = jnp.zeros((SIDE, CH), F32)
        hf[t, 21, SIDE:24, :] = jnp.zeros((EDGE, CH), F32)
    for slot in range(BLOCK):
        for half in range(2):
            xf[slot, half, 72:88, :] = jnp.zeros((EDGE, CH), F32)
            xf[slot, half, 21 * PITCH + SIDE:21 * PITCH + 24, :] = jnp.zeros((EDGE, CH), F32)

    @pl.when(row == 0)
    def _():
        for t in range(steps):
            hf[t, 1, SIDE:PITCH, :] = jnp.zeros((72, CH), F32)
            hf[t, 2, 0:PITCH, :] = jnp.zeros((PITCH, CH), F32)
            hf[t, 3, 0:SIDE, :] = jnp.zeros((SIDE, CH), F32)
            fs[t, 0:2] = jnp.zeros((2, WIDE, CIN), BF16)
            fl[t, 0:2] = jnp.zeros((2, SIDE, CIN), BF16)
            fr[t, 0:2] = jnp.zeros((2, SIDE, CIN), BF16)
        for s in range(2):
            hl[s, 0:2] = jnp.zeros((2, SIDE, CH), F32)
            hr[s, 0:2] = jnp.zeros((2, SIDE, CH), F32)

    @pl.when(row == n_rows - 1)
    def _():
        for t in range(steps):
            hf[t, 19, SIDE:PITCH, :] = jnp.zeros((72, CH), F32)
            hf[t, TALL, 0:PITCH, :] = jnp.zeros((PITCH, CH), F32)
            hf[t, 21, 0:SIDE, :] = jnp.zeros((SIDE, CH), F32)
            fs[t, 18:TALL] = jnp.zeros((2, WIDE, CIN), BF16)
            fl[t, 18:TALL] = jnp.zeros((2, SIDE, CIN), BF16)
            fr[t, 18:TALL] = jnp.zeros((2, SIDE, CIN), BF16)
        for s in range(2):
            hl[s, 18:TALL] = jnp.zeros((2, SIDE, CH), F32)
            hr[s, 18:TALL] = jnp.zeros((2, SIDE, CH), F32)

    @pl.when(col == 0)
    def _():
        for t in range(steps):
            fl[t] = jnp.zeros((TALL, SIDE, CIN), BF16)
        hl[...] = jnp.zeros((2, TALL, SIDE, CH), F32)

    @pl.when(col == n_cols - 1)
    def _():
        for t in range(steps):
            fr[t] = jnp.zeros((TALL, SIDE, CIN), BF16)
        hr[...] = jnp.zeros((2, TALL, SIDE, CH), F32)

    for c in range(3):
        vb[c, 1616:1696, :] = jnp.zeros((PITCH, CH), BF16)
    rh[2 * PITCH - SIDE:2 * PITCH, :] = jnp.zeros((SIDE, CH), F32)
    rh[TALL * PITCH + EDGE:TALL * PITCH + 24, :] = jnp.zeros((SIDE, CH), F32)

    def two_rows(dst, src, depth, lanes):
        zero = jnp.zeros((depth, CH), BF16)
        for c in range(3):
            for a in range(4):
                i = (a * 3 + c) * depth
                dst[i:i + depth, 0:CH] = src[a * 3 + c, :, lanes] if a < 3 else zero
                dst[i:i + depth, CH:2 * CH] = src[a * 3 + c - 3, :, lanes] if a > 0 else zero

    weights[0].wait()
    two_rows(wxn, wx, CIN, slice(2 * CH, 3 * CH))

    def take(ref, boxes):
        parts = [ref[k0:k1, j0:j1, :] for k0, k1, j0, j1 in boxes]
        return jnp.concatenate([x.reshape(-1, x.shape[-1]) for x in parts], axis=0)

    def put(ref, boxes, value):
        at = 0
        for k0, k1, j0, j1 in boxes:
            size = (k1 - k0) * (j1 - j0)
            ref[k0:k1, j0:j1, :] = value[at:at + size].reshape(k1 - k0, j1 - j0, value.shape[-1])
            at += size

    def two_row_patches(ref, depth, boxes):
        taps = []
        for a in range(4):
            lead = 1 + a // 2
            for c in range(3):
                rows = ref.at[c].reshape(BLOCKS // 2, 2, PITCH, depth)
                parts = [rows[y0 + lead:y1 + lead, a % 2, j0:j1, :] for y0, y1, j0, j1 in boxes]
                taps.append(jnp.concatenate([x.reshape(-1, depth) for x in parts], axis=0))
        return jnp.concatenate(taps, axis=1)

    def matmul(lhs, w):
        return jnp.dot(lhs, w, preferred_element_type=F32)

    def shifted(dst, src, lo, hi):
        for c in range(3):
            dst[c, lo:hi, :] = src[lo - 1 + c:hi - 1 + c, :].astype(BF16)

    halves = [(half, slice(half * CH, half * CH + CH)) for half in range(2)]

    def prep_core(t, slot):
        for half, lanes in halves:
            cells = xf.at[slot, half].reshape(BLOCKS, PITCH, CH)
            cells[3:19, EDGE:PITCH, :] = fs[t, 2:18, :, lanes].astype(F32)
            for c in range(3):
                fx[slot, c, 3:19, 32:WIDE, lanes] = cells[3:19, 31 + c:63 + c, :].astype(BF16)

    def prep_rim(t, slot):
        for half, lanes in halves:
            flat = xf.at[slot, half]
            cells = flat.reshape(BLOCKS, PITCH, CH)
            cells[1:3, EDGE:PITCH, :] = fs[t, 0:2, :, lanes].astype(F32)
            cells[19:21, EDGE:PITCH, :] = fs[t, 18:TALL, :, lanes].astype(F32)
            cells[1:21, SIDE:EDGE, :] = fl[t, :, :, lanes].astype(F32)
            cells[2:22, 0:SIDE, :] = fr[t, :, :, lanes].astype(F32)
            for c in range(3):
                out = fx.at[slot, c]
                for k in OUTER:
                    first = PITCH * k - 1 + c
                    out[k, :, lanes] = flat[first:first + PITCH, :].astype(BF16)
                out[21, 0:EDGE, lanes] = flat[PITCH * 21 - 1 + c:PITCH * 21 - 1 + c + EDGE, :].astype(BF16)
                for k in range(3, 19):
                    first = PITCH * k - 1 + c
                    out[k, 0:32, lanes] = flat[first:first + 32, :].astype(BF16)
                    out[k, WIDE:PITCH, lanes] = flat[first + WIDE:first + PITCH, :].astype(BF16)

    def gates(slot, chunks):
        bias_zr = bias[0:2 * CH][None, :]
        wzr = wx[:, :, 0:2 * CH].reshape(9 * CIN, 2 * CH)
        for boxes in chunks:
            taps = [take(fx.at[slot, c], [(k0 + a, k1 + a, j0, j1) for k0, k1, j0, j1 in boxes]) for a in (-1, 0, 1) for c in range(3)]
            put(gz.at[slot], boxes, matmul(jnp.concatenate(taps, axis=1), wzr) + bias_zr)

    def cand_gates(slot, chunks):
        bias_n = bias[2 * CH:3 * CH]
        bias_n = jnp.concatenate([bias_n, bias_n])[None, :]
        for boxes in chunks:
            put(gn.at[slot], boxes, matmul(two_row_patches(fx.at[slot], CIN, boxes), wxn[...]) + bias_n)

    def zr_gates(slot, h_flat, chunks):
        whzr = wh[...].reshape(9 * CH, 2 * CH)
        base = gz.at[slot].reshape(CELLS, 2 * CH)
        for lo, size in chunks:
            here = slice(lo, lo + size)
            taps = [ub[c, lo + a:lo + a + size, :] for a in (-PITCH, 0, PITCH) for c in range(3)]
            gate = 0.5 * jnp.tanh(0.5 * (matmul(jnp.concatenate(taps, axis=1), whzr) + base[here, :])) + 0.5
            zb[here, :] = gate[:, 0:CH]
            rh[here, :] = gate[:, CH:2 * CH] * h_flat[here, :]

    left_edge = col == 0
    right_edge = col == n_cols - 1

    def new_state(t, slot, chunks):
        def rows_of(ref, n):
            return ref.reshape(n // 2, 2, ref.shape[-2], CH)
        old, new = rows_of(hf.at[t].reshape(BLOCKS, PITCH, CH), BLOCKS), rows_of(hf.at[t + 1].reshape(BLOCKS, PITCH, CH), BLOCKS)
        update = zb.reshape(BLOCKS // 2, 2, PITCH, CH)
        seq, final = rows_of(h_seq.at[t, 0], EDGE), rows_of(h_last.at[0], EDGE)
        for boxes in chunks:
            cand = jnp.tanh(matmul(two_row_patches(vb, CH, boxes), whn[...]) + take(gn.at[slot], boxes))
            at = 0
            for y0, y1, j0, j1 in boxes:
                n = (y1 - y0) * (j1 - j0)
                for odd in range(2):
                    if y0 == SIDE and odd:
                        continue
                    ks = slice(y0 + 1 + odd, y1 + 1 + odd)
                    par = 1 - odd
                    z = update[ks, par, j0:j1, :]
                    c = cand[at:at + n, odd * CH:odd * CH + CH].reshape(y1 - y0, j1 - j0, CH)
                    h_new = (1.0 - z) * c + z * old[ks, par, j0:j1, :]
                    lo = max(j0, EDGE)
                    if lo < j1:
                        main = h_new[:, lo - j0:]
                        seq[y0:y1, odd, lo - EDGE:j1 - EDGE, :] = main.astype(BF16)
                        final[y0:y1, odd, lo - EDGE:j1 - EDGE, :] = main
                        new[ks, par, lo:j1, :] = main
                    if j0 == 0 and y0 < SIDE:
                        new[ks, par, SIDE:EDGE, :] = jnp.where(left_edge, 0.0, h_new[:, SIDE:EDGE])
                    if j0 == 0 and (y0 or odd):
                        new[ks, par, 0:SIDE, :] = jnp.where(right_edge, 0.0, h_new[:, 0:SIDE])
                at += n

    def block(b, carry):
        t0 = b * BLOCK

        @pl.when(b == 0)
        def _():
            for t in range(1, BLOCK):
                frame_copy(t).wait()

        @pl.when(b > 0)
        def _():
            for j in range(BLOCK):
                frame_copy(t0 + j).wait()

        for j in range(BLOCK):
            prep_core(t0 + j, j)
            gates(j, GATE_CORE)
        for j in range(BLOCK - 1):
            cand_gates(j, [CAND_CORE[0] + CAND_CORE[1]])
        cand_gates(BLOCK - 1, CAND_CORE)

        @pl.when(b == 0)
        def _():
            weights[1].wait()
            weights[2].wait()
            two_rows(whn, whr, CH, slice(0, CH))

        finish(lambda i: frame_xfer(t0, i))
        prep_rim(t0, 0)
        gates(0, GATE_RIM)
        cand_gates(0, CAND_RIM)
        finish(lambda i: state_xfer(t0, i, b))
        hf[t0, 1:21, SIDE:EDGE, :] = hl[b]
        hf[t0, 2:22, 0:SIDE, :] = hr[b]
        h_flat = hf.at[t0].reshape(CELLS, CH)
        shifted(ub, h_flat, PITCH, 1696)
        zr_gates(0, h_flat, ZR_CORE + ZR_RIM)
        shifted(vb, rh, 160, 1616)
        new_state(t0, 0, N_CORE + N_RIM)
        start(lambda i: state_xfer(t0 + 1, i, None), True)

        for j in range(1, BLOCK):
            t = t0 + j
            finish(lambda i: frame_xfer(t, i))
            h_flat = hf.at[t].reshape(CELLS, CH)
            prep_rim(t, j)
            shifted(ub, h_flat, 256, 1520)
            ends = h_flat[1520:1528, :]
            for c, x in enumerate((h_flat[1519:1527, :], ends, pltpu.roll(ends, SIDE - 1, 0))):
                ub[c, 1520:1528, :] = x.astype(BF16)
            gates(j, GATE_RIM)
            zr_gates(j, h_flat, ZR_CORE)
            shifted(vb, rh, 480, 1440)
            cand_gates(j, CAND_RIM)
            new_state(t, j, N_CORE)
            finish(lambda i: state_xfer(t, i, None), True)
            shifted(ub, h_flat, PITCH, 256)
            shifted(ub, h_flat, 1520, 1696)
            zr_gates(j, h_flat, ZR_RIM)
            shifted(vb, rh, 160, 480)
            shifted(vb, rh, 1440, 1616)
            new_state(t, j, N_RIM)
            if j < BLOCK - 1:
                start(lambda i: state_xfer(t + 1, i, None), True)
            else:
                @pl.when(b == 0)
                def _():
                    start(lambda i: state_xfer(t + 1, i, 1))
        return carry

    lax.fori_loop(0, steps // BLOCK, block, 0)


def solution(mesh):
    n_rows = mesh.shape['rows']
    n_cols = mesh.shape['cols']
    frame_spec = P(None, 'batch', 'rows', 'cols', None)
    state_spec = P('batch', 'rows', 'cols', None)

    def local_fn(frames, h_init, w_x, w_hzr, w_hn, gate_bias):
        steps = frames.shape[0]
        any_spec = pl.BlockSpec(memory_space=pl.ANY)
        vmem = pltpu.VMEM
        dma = pltpu.SemaphoreType.DMA
        return pl.pallas_call(
            functools.partial(kernel, n_rows, n_cols, steps),
            out_shape=(vmem((steps, 1, EDGE, WIDE, CH), BF16), vmem((1, EDGE, WIDE, CH), F32)),
            in_specs=[any_spec] * 5 + [pl.BlockSpec(memory_space=pltpu.VMEM)],
            out_specs=(pl.BlockSpec(memory_space=vmem), pl.BlockSpec(memory_space=vmem)),
            scratch_shapes=[
                vmem((steps + 1, BLOCKS, PITCH, CH), F32),
                vmem((2, TALL, SIDE, CH), F32),
                vmem((2, TALL, SIDE, CH), F32),
                vmem((steps, TALL, WIDE, CIN), BF16),
                vmem((steps, TALL, SIDE, CIN), BF16),
                vmem((steps, TALL, SIDE, CIN), BF16),
                vmem((BLOCK, 2, BLOCKS * PITCH, CH), F32),
                vmem((BLOCK, 3, BLOCKS, PITCH, CIN), BF16),
                vmem((3, CELLS, CH), BF16),
                vmem((BLOCKS * PITCH, CH), F32),
                vmem((3, CELLS, CH), BF16),
                vmem((CELLS, CH), F32),
                vmem((BLOCK, BLOCKS, PITCH, CIN), F32),
                vmem((BLOCK, 9, PITCH, CIN), F32),
                vmem((9, CIN, 384), BF16),
                vmem((12 * CIN, CIN), BF16),
                vmem((9, CH, CIN), BF16),
                vmem((12 * CH, CIN), BF16),
                vmem((9, CH, CH), BF16),
                dma((4,)), dma((steps,)),
                dma((steps, SIDE)), dma((steps, SIDE)), dma((steps, SIDE)), dma((steps, SIDE)),
            ],
            compiler_params=pltpu.CompilerParams(collective_id=0, has_side_effects=True, vmem_limit_bytes=60 * 1024 * 1024),
        )(frames, h_init, w_x.reshape(9, CIN, 384), w_hzr.reshape(9, CH, CIN), w_hn.reshape(9, CH, CH), gate_bias)

    return jax.shard_map(local_fn, mesh=mesh, in_specs=(frame_spec, state_spec, P(), P(), P(), P()), out_specs=(frame_spec, state_spec), check_vma=False)
```

time: 282 us -> 43.7 us (0.15); the launches traced: 278 us -> 43.6 us
  starting transfers between devices: 157 us -> 0 us
  waiting for transfers between devices: 43.9 us -> 0 us
  Pallas kernels: 0 us -> 41 us
  matrix products: 37.4 us -> 0 us
  local copies, waits for them, and re-layouts: 27 us -> 1.94 us
  other arithmetic: 9.88 us -> 0 us
    ppermute x52 -> x0, starting transfers between devices: 157 us -> none  [the longest x13 41.9 us: with_halo(): lax.ppermute(tile[..., tile_h - width:, :, :], 'rows', down_pairs)]
    ppermute x52 -> x0, waiting for transfers between devices: 43.9 us -> none  [the longest x13 34.7 us: with_halo(): lax.ppermute(tall_tile[..., tile_w - width:, :], 'cols', right_pairs)]
    pallas_call x0 -> x1, Pallas kernels: none -> 41 us  [local_fn(): pl.pallas_call(functools.partial(kernel, n_rows, n_cols, steps), out_shap...]
    dot_general x18 -> x0, matrix products: 37.4 us -> none  [im2col_conv(): jnp.einsum('...k,kg->...g', patches, w_mat, preferred_element_type=jnp.fl...]
    while x138 -> x0, local copies, waits for them, and re-layouts: 11.4 us -> none
    concatenate x25 -> x0, other arithmetic: 7.18 us -> none  [the longest x13 6.94 us: with_halo(): return jnp.concatenate([from_left, tall_tile, from_right], axis=-2)]
    squeeze x6 -> x0, local copies, waits for them, and re-layouts: 6.84 us -> none  [local_fn(): h_last, h_seq = lax.scan(one_step, h_init, frames_pad)]
    unnamed x14 -> x2, local copies, waits for them, and re-layouts: 4.87 us -> 1.94 us
  transfers between devices with their start and end apart: 52 -> 0, of which waited for: 22 -> 0; matrix products, arithmetic and copies ran while one was open for 11% -> 0% of each run, Pallas kernels for 0% -> 0%
where the time goes in v3:
time: 43.7 us; the launch traced here: 43.6 us
  Pallas kernels  41 us (94%)
  local copies, waits for them, and re-layouts  1.94 us (4%)
  between operations  0.64 us (1%)
    pallas_call x1, Pallas kernels, local_fn(): pl.pallas_call(functools.partial(kernel, n_rows, n_cols, steps), out_shap...  41 us
    unnamed x2, local copies, waits for them, and re-layouts  1.94 us

profile of v3, /device:TPU:99, one launch (start us, length us, event | category | flops | bytes accessed | tf_op | source)
XLA Modules:
  0.0 43.6 jit_solution(18166933836491347528)
XLA Ops:
  0.6 41.0 %shard_map.77 = (bf16[6,1,16,64,128]{4,3,2,1,0:T(8,128)(2,1)S(1)}, f32[1,16,64,128]{3,2,1,0:T(8,128)S(1)}) custom-call(bf16[6,1,16,64,256]{4,3,2,1,0:T(8,128)(2,1)} %frames.1, f32[1,16,64,128]{3,2,1,0:T(8,128)} %h_init.1, bf16[9,256,384]{2,1,0:T(8,128)(2,1)} %bitcast.3, bf16[9,128,256]{2,1,0:T(8,128)(2,1)} %bitcast.4, bf16[9,128,128]{2,1,0:T(8,128)(2,1)} %bitcast.5, ...), custom_call_target="tpu_custom_call" | custom-call | tf_op jit(solution)/shard_map/pallas_call | solution.py:399
  41.6 1.1 %copy.10 = bf16[6,1,16,64,128]{4,3,2,1,0:T(8,128)(2,1)} copy(bf16[6,1,16,64,128]{4,3,2,1,0:T(8,128)(2,1)S(1)} %get-tuple-element.2) | data formatting | bytes 3145728
  42.8 0.8 %copy.11 = f32[1,16,64,128]{3,2,1,0:T(8,128)} copy(f32[1,16,64,128]{3,2,1,0:T(8,128)S(1)} %get-tuple-element.3) | data formatting | bytes 1048576

commit v4 on v3

--- a/solution.py
+++ b/solution.py
@@ -366,11 +366,11 @@
             zr_gates(j, h_flat, ZR_CORE)
             shifted(vb, rh, 480, 1440)
             cand_gates(j, CAND_RIM)
-            new_state(t, j, N_CORE)
             finish(lambda i: state_xfer(t, i, None), True)
             shifted(ub, h_flat, PITCH, 256)
             shifted(ub, h_flat, 1520, 1696)
             zr_gates(j, h_flat, ZR_RIM)
+            new_state(t, j, N_CORE[::-1])
             shifted(vb, rh, 160, 480)
             shifted(vb, rh, 1440, 1616)
             new_state(t, j, N_RIM)

time: 43.7 us -> 43.5 us (level)
  no operation moved by 1% of the time
where the time goes in v4:
time: 43.5 us; the launch traced here: 43.4 us
  Pallas kernels  40.8 us (94%)
  local copies, waits for them, and re-layouts  1.94 us (4%)
  between operations  0.64 us (1%)
    pallas_call x1, Pallas kernels, local_fn(): pl.pallas_call(functools.partial(kernel, n_rows, n_cols, steps), out_shap...  40.8 us
    unnamed x2, local copies, waits for them, and re-layouts  1.94 us

profile of v4, /device:TPU:99, one launch (start us, length us, event | category | flops | bytes accessed | tf_op | source)
XLA Modules:
  0.0 43.4 jit_solution(6250868558715748245)
XLA Ops:
  0.6 40.8 %shard_map.77 = (bf16[6,1,16,64,128]{4,3,2,1,0:T(8,128)(2,1)S(1)}, f32[1,16,64,128]{3,2,1,0:T(8,128)S(1)}) custom-call(bf16[6,1,16,64,256]{4,3,2,1,0:T(8,128)(2,1)} %frames.1, f32[1,16,64,128]{3,2,1,0:T(8,128)} %h_init.1, bf16[9,256,384]{2,1,0:T(8,128)(2,1)} %bitcast.3, bf16[9,128,256]{2,1,0:T(8,128)(2,1)} %bitcast.4, bf16[9,128,128]{2,1,0:T(8,128)(2,1)} %bitcast.5, ...), custom_call_target="tpu_custom_call" | custom-call | tf_op jit(solution)/shard_map/pallas_call | solution.py:399
  41.4 1.1 %copy.10 = bf16[6,1,16,64,128]{4,3,2,1,0:T(8,128)(2,1)} copy(bf16[6,1,16,64,128]{4,3,2,1,0:T(8,128)(2,1)S(1)} %get-tuple-element.2) | data formatting | bytes 3145728
  42.6 0.8 %copy.11 = f32[1,16,64,128]{3,2,1,0:T(8,128)} copy(f32[1,16,64,128]{3,2,1,0:T(8,128)S(1)} %get-tuple-element.3) | data formatting | bytes 1048576

commit v5 on v4

--- a/solution.py
+++ b/solution.py
@@ -133,7 +133,6 @@
         start(lambda i: frame_xfer(t, i))
         return carry
 
-    lax.fori_loop(1, steps, start_rest, 0)
     for t in range(BLOCK, steps):
         frame_copy(t).start()
 
@@ -335,6 +334,7 @@
 
         @pl.when(b == 0)
         def _():
+            lax.fori_loop(1, steps, start_rest, 0)
             weights[1].wait()
             weights[2].wait()
             two_rows(whn, whr, CH, slice(0, CH))

time: 43.5 us -> 42.9 us (0.986)
  Pallas kernels: 40.8 us -> 40.2 us
    pallas_call x1, Pallas kernels: 40.8 us -> 40.2 us  [local_fn(): pl.pallas_call(functools.partial(kernel, n_rows, n_cols, steps), out_shap...]
where the time goes in v5:
time: 42.9 us; the launch traced here: 42.8 us
  Pallas kernels  40.2 us (94%)
  local copies, waits for them, and re-layouts  1.94 us (5%)
  between operations  0.64 us (1%)
    pallas_call x1, Pallas kernels, local_fn(): pl.pallas_call(functools.partial(kernel, n_rows, n_cols, steps), out_shap...  40.2 us
    unnamed x2, local copies, waits for them, and re-layouts  1.94 us

profile of v5, /device:TPU:99, one launch (start us, length us, event | category | flops | bytes accessed | tf_op | source)
XLA Modules:
  0.0 42.8 jit_solution(16401834307517028076)
XLA Ops:
  0.6 40.2 %shard_map.77 = (bf16[6,1,16,64,128]{4,3,2,1,0:T(8,128)(2,1)S(1)}, f32[1,16,64,128]{3,2,1,0:T(8,128)S(1)}) custom-call(bf16[6,1,16,64,256]{4,3,2,1,0:T(8,128)(2,1)} %frames.1, f32[1,16,64,128]{3,2,1,0:T(8,128)} %h_init.1, bf16[9,256,384]{2,1,0:T(8,128)(2,1)} %bitcast.3, bf16[9,128,256]{2,1,0:T(8,128)(2,1)} %bitcast.4, bf16[9,128,128]{2,1,0:T(8,128)(2,1)} %bitcast.5, ...), custom_call_target="tpu_custom_call" | custom-call | tf_op jit(solution)/shard_map/pallas_call | solution.py:399
  40.9 1.1 %copy.10 = bf16[6,1,16,64,128]{4,3,2,1,0:T(8,128)(2,1)} copy(bf16[6,1,16,64,128]{4,3,2,1,0:T(8,128)(2,1)S(1)} %get-tuple-element.2) | data formatting | bytes 3145728
  42.0 0.8 %copy.11 = f32[1,16,64,128]{3,2,1,0:T(8,128)} copy(f32[1,16,64,128]{3,2,1,0:T(8,128)S(1)} %get-tuple-element.3) | data formatting | bytes 1048576
